TPU v7x, 32 devices: a whole 2x2x4 slice. The times are simulated.
32 devices in a mesh: ma: 8 (over z, y), pb: 4 (over x, core).
Axes of the slice: x: 2, y: 2, z: 4, core: 2. Of those that a mesh axis runs over, the one named last changes fastest.
Arguments:
- coefs: float32 [512, 1056, 64], P('ma', 'pb'), may hold values from -6 to 6
- legendre: float32 [512, 1056, 4, 256], P('ma', None, 'pb'), may hold values from -0.25 to 0.25
- quad_weight: float32 [4, 256], P('pb'), may hold values from 0.3 to 3
- pair_of_slot: int32 [512], replicated, may hold values from 0 to 511, each once
- tracers: float32 [12, 2, 1024, 2048], P(None, None, ('ma', 'pb')), may hold values from 0 to 2
- heat_rate: float32 [12, 2], replicated, may hold values from -1.75 to 1.75
Outputs:
- spec_tendency: float32 [512, 1056, 64], P('ma', 'pb')
- tracers_new: float32 [12, 2, 1024, 2048], P(None, None, ('ma', 'pb'))
Inputs may be any that keep to these rules, and one draw needn't show every extreme that they name: Each pair number appears once; slot s holds the orders pair_of_slot[s] and 1023 - pair_of_slot[s].
All inputs are finite; a program needn't handle non-finite values.
Results may differ from a plain program's by a relative error of at most 0.00007.
Values sent between devices are 32-bit elements; how exact they have to be, the bound alone decides.
A program may use at most 320 MiB of HBM per device.

v0:
```python
import math

import jax
import jax.numpy as jnp
from jax import lax
from jax.experimental import pallas as pl
from jax.experimental.pallas import tpu as pltpu
from jax.sharding import PartitionSpec as P

M = 1024
NLAT = 1024
NLON = 2048
LAYER_TOTAL = 8
NF = 4
NTR = 12
TLEV = 2
PAIRS = 512


COURANT = 0.15
DRAG_COEFFICIENT = 0.2
MOISTURE_SOURCE = 0.3
RAINFALL_FACTOR = 0.2
HIGH = lax.Precision.HIGH

HALO = 3
EDGE = 8


def halo_rows(block, axes, dim, width):
    count = lax.axis_size(axes)
    forward = [(i, i + 1) for i in range(count - 1)]
    backward = [(target, source) for source, target in forward]
    low = lax.ppermute(
        lax.slice_in_dim(block, block.shape[dim] - width, None, axis=dim), axes, forward
    )
    high = lax.ppermute(lax.slice_in_dim(block, 0, width, axis=dim), axes, backward)
    return low, high


def split_orders(pair_ids):
    low_even = pair_ids % 2 == 0
    even = jnp.where(low_even, pair_ids, M - 1 - pair_ids)
    return low_even, even, M - 1 - even


def half_tables(orders, points):
    step = 128
    coarse_ids = jnp.arange(points // step, dtype=jnp.int32) * step
    fine_ids = jnp.arange(step, dtype=jnp.int32)
    unit = 2.0 * math.pi / NLON
    coarse = (orders[:, None] * coarse_ids[None, :] % NLON).astype(jnp.float32) * unit
    fine = (orders[:, None] * fine_ids[None, :] % NLON).astype(jnp.float32) * unit
    factor = 1.0 / math.sqrt(NLON)
    cc, sc = lax.optimization_barrier((jnp.cos(coarse) * factor, jnp.sin(coarse) * factor))
    cf, sf = lax.optimization_barrier((jnp.cos(fine), jnp.sin(fine)))
    cos = [cc[:, a : a + 1] * cf - sc[:, a : a + 1] * sf for a in range(points // step)]
    sin = [-(sc[:, a : a + 1] * cf + cc[:, a : a + 1] * sf) for a in range(points // step)]
    return jnp.stack([jnp.concatenate(cos, axis=1), jnp.concatenate(sin, axis=1)], axis=0)


def row_masks(pair_ids, row_count):
    row_ids = jnp.arange(row_count, dtype=jnp.int32)
    bounds = (M - pair_ids)[:, None]
    low_rows = row_ids[None, :] < bounds
    high_rows = (row_ids[None, :] >= bounds) & (row_ids[None, :] <= M)
    low_even = (pair_ids % 2 == 0)[:, None]
    even_rows = (low_even & low_rows) | (~low_even & high_rows)
    odd_rows = (low_even & high_rows) | (~low_even & low_rows)
    return (even_rows, odd_rows)


def transport_kernel(
    first_ref, rate_ref, q_ref, ql_ref, qh_ref, u_ref, ul_ref, uh_ref, w_ref, wl_ref, wh_ref,
    out_ref, heat_ref, pad, ap, an, bp, bn,
):
    rows = q_ref.shape[2]
    total = rows + 2 * EDGE
    lons = q_ref.shape[3]
    level = pl.program_id(0)
    tracer = pl.program_id(1)

    def fill(mid, low, high):
        pad[EDGE : EDGE + rows, :] = mid
        pad[EDGE - HALO : EDGE, :] = low
        pad[EDGE + rows : EDGE + rows + HALO, :] = high

    @pl.when(tracer == 0)
    def _():
        fill(u_ref[0], ul_ref[0], uh_ref[0])
        u = pad[...]
        face = (0.5 * COURANT) * (u + pltpu.roll(u, lons - 1, 1))
        ap[...] = jnp.maximum(face, 0.0)
        an[...] = jnp.minimum(face, 0.0)
        fill(w_ref[0], wl_ref[0], wh_ref[0])
        w = pad[...]
        face = (-0.5 * COURANT) * (w + pltpu.roll(w, total - 1, 0))
        upper = first_ref[0] - EDGE + lax.broadcasted_iota(jnp.int32, (total, lons), 0)
        inside = (upper >= 0) & (upper <= NLAT - 2)
        bp[...] = jnp.where(inside, jnp.maximum(face, 0.0), 0.0)
        bn[...] = jnp.where(inside, jnp.minimum(face, 0.0), 0.0)

    def step(q):
        east = ap[...] * q + an[...] * pltpu.roll(q, lons - 1, 1)
        south = bp[...] * q + bn[...] * pltpu.roll(q, total - 1, 0)
        return q - ((east - pltpu.roll(east, 1, 1)) + (south - pltpu.roll(south, 1, 0)))

    fill(q_ref[0, 0], ql_ref[0, 0], qh_ref[0, 0])
    q = pad[...]
    second = 0.75 * q + 0.25 * step(step(q))
    third = step(second)[EDGE : EDGE + rows]
    new = q_ref[0, 0] * (1.0 / 3.0) + (2.0 / 3.0) * third
    out_ref[0, 0] = new
    warm = rate_ref[tracer, level] * new

    @pl.when(tracer == 0)
    def _():
        heat_ref[0] = warm

    @pl.when(tracer > 0)
    def _():
        heat_ref[0] += warm


def transport(first_row, heat_rate, tracers, low, high, wind, wind_low, wind_high):
    count, levels, rows, lons = tracers.shape
    total = rows + 2 * EDGE

    def tracer_spec(height):
        return pl.BlockSpec((1, 1, height, lons), lambda l, k: (k, l, 0, 0))

    def wind_spec(height):
        return pl.BlockSpec((1, height, lons), lambda l, k: (l, 0, 0))

    smem = pl.BlockSpec(memory_space=pltpu.SMEM)
    return pl.pallas_call(
        transport_kernel,
        grid=(levels, count),
        in_specs=[smem, smem]
        + [tracer_spec(rows), tracer_spec(HALO), tracer_spec(HALO)]
        + [wind_spec(rows), wind_spec(HALO), wind_spec(HALO)] * 2,
        out_specs=[tracer_spec(rows), wind_spec(rows)],
        out_shape=[
            jax.ShapeDtypeStruct(tracers.shape, tracers.dtype),
            jax.ShapeDtypeStruct((levels, rows, lons), tracers.dtype),
        ],
        scratch_shapes=[pltpu.VMEM((total, lons), jnp.float32)] * 5,
        compiler_params=pltpu.CompilerParams(
            dimension_semantics=("arbitrary", "arbitrary"), vmem_limit_bytes=40 * 1024 * 1024
        ),
    )(
        first_row.reshape(1), heat_rate, tracers, low, high,
        wind[0], wind_low[0], wind_high[0], wind[1], wind_low[1], wind_high[1],
    )


def shards(coefs, legendre, quad_weight, pair_of_slot, tracers, heat_rate):
    slot_count = coefs.shape[0]
    columns = coefs.shape[2]
    quarter = legendre.shape[3]
    half = NLON // 2
    part = NF * LAYER_TOTAL
    legendre_rows = legendre.reshape(slot_count, legendre.shape[1], quarter)
    own_pairs = lax.dynamic_slice_in_dim(
        pair_of_slot, lax.axis_index("ma") * slot_count, slot_count, 0
    )
    low, high = halo_rows(tracers, ("ma", "pb"), 2, HALO)
    row_piece = lax.all_gather(coefs, "pb", axis=1, tiled=True)
    even_rows, odd_rows = row_masks(own_pairs, row_piece.shape[1])
    even_orders = split_orders(own_pairs)[1]
    even_weight = jnp.where(even_orders == 0, 1.0, 2.0).astype(jnp.float32)[:, None, None]
    masked = jnp.concatenate(
        [
            jnp.where(even_rows[:, :, None], row_piece * even_weight, 0.0),
            jnp.where(odd_rows[:, :, None], row_piece * 2.0, 0.0),
        ],
        axis=2,
    )
    legendre_sum = jnp.einsum("srl,src->slc", legendre_rows, masked, precision=HIGH)
    bands = lax.all_to_all(legendre_sum, "ma", split_axis=1, concat_axis=0, tiled=True)
    band_rows = bands.shape[1]
    _, even_all, odd_all = split_orders(pair_of_slot)
    even_table = half_tables(even_all, half)
    odd_table = half_tables(odd_all, half)
    spectral = bands.reshape(PAIRS, band_rows, 2, 2, part)
    even_sum = jnp.einsum("sjpc,psi->jci", spectral[:, :, 0], even_table, precision=HIGH)
    odd_sum = jnp.einsum("sjpc,psi->jci", spectral[:, :, 1], odd_table, precision=HIGH)
    field = jnp.concatenate([even_sum + odd_sum, even_sum - odd_sum], axis=2)
    wind = jnp.stack(
        [
            jnp.transpose(field[:, 0:TLEV, :], (1, 0, 2)),
            jnp.transpose(field[:, LAYER_TOTAL : LAYER_TOTAL + TLEV, :], (1, 0, 2)),
        ],
        axis=0,
    )
    wind_low, wind_high = halo_rows(wind, ("ma", "pb"), 2, HALO)
    first_row = (lax.axis_index(("ma", "pb")) * band_rows).astype(jnp.int32)
    new_tracers, heating = transport(
        first_row, heat_rate, tracers, low, high, wind, wind_low, wind_high
    )
    heating = jnp.transpose(heating, (1, 0, 2))
    u = field[:, 0:LAYER_TOTAL]
    v = field[:, LAYER_TOTAL : 2 * LAYER_TOTAL]
    t = field[:, 2 * LAYER_TOTAL : 3 * LAYER_TOTAL]
    q = field[:, 3 * LAYER_TOTAL : 4 * LAYER_TOTAL]
    speed = jnp.sqrt(u * u + v * v + 1.0)
    warming = jnp.pad(heating, ((0, 0), (0, LAYER_TOTAL - TLEV), (0, 0)))
    moist = MOISTURE_SOURCE * t * q
    tendency = jnp.concatenate(
        [
            -DRAG_COEFFICIENT * speed * u,
            -DRAG_COEFFICIENT * speed * v,
            warming - moist,
            moist - RAINFALL_FACTOR * speed * q,
        ],
        axis=1,
    )
    near = tendency[:, :, :half]
    far = tendency[:, :, half:]
    even_fourier = jnp.einsum("jci,psi->sjpc", near + far, even_table, precision=HIGH)
    odd_fourier = jnp.einsum("jci,psi->sjpc", near - far, odd_table, precision=HIGH)
    fourier = jnp.concatenate(
        [
            even_fourier.reshape(PAIRS, band_rows, columns),
            odd_fourier.reshape(PAIRS, band_rows, columns),
        ],
        axis=2,
    )
    by_orders = lax.all_to_all(fourier, "ma", split_axis=0, concat_axis=1, tiled=True)
    weighted = by_orders * quad_weight.reshape(quarter)[None, :, None]
    row_sums = jnp.einsum("srl,slc->rsc", legendre_rows, weighted, precision=HIGH)
    summed = lax.psum_scatter(
        jnp.where(even_rows.T[:, :, None], row_sums[:, :, :columns], 0.0)
        + jnp.where(odd_rows.T[:, :, None], row_sums[:, :, columns:], 0.0),
        "pb",
        scatter_dimension=0,
        tiled=True,
    )
    return (jnp.transpose(summed, (1, 0, 2)), new_tracers)


def solution(mesh):
    in_specs = (
        P("ma", "pb", None),
        P("ma", None, "pb", None),
        P("pb", None),
        P(),
        P(None, None, ("ma", "pb"), None),
        P(),
    )
    out_specs = (P("ma", "pb", None), P(None, None, ("ma", "pb"), None))
    return jax.shard_map(shards, mesh=mesh, in_specs=in_specs, out_specs=out_specs, check_vma=False)
```

profile of v0, /device:TPU:12, one launch (start us, length us, event | category | flops | bytes accessed | tf_op | source)
XLA Modules:
  0.0 1209.6 jit_solution(11022951716136289504)
XLA Ops:
  7.2 8.8 copy.50
  18.3 208.8 %all-gather.2.cloned.1.call-done = f32[64,1056,64]{2,1,0:T(8,128)} async-done(((f32[64,264,64]{2,1,0:T(8,128)}), f32[64,1056,64]{2,1,0:T(8,128)}) %all-gather.2.cloned.1.call-update) | async-done | bytes 17301520 | tf_op jit(solution)/shard_map/all_gather | solution.py:168
  227.1 34.9 %multiply_select_fusion.1 = (f32[64,1056,64]{2,1,0:T(8,128)}, f32[64,1056,64]{2,1,0:T(8,128)}) fusion(f32[64,1056,64]{2,1,0:T(8,128)} %all-gather.2.cloned.1.call-done, f32[64]{0:T(128)S(1)} %get-tuple-element.34, pred[64,1056]{1,0:T(8,128)(4,1)S(1)} %get-tuple-element.123, pred[64,1056]{1,0:T(8,128)(4,1)S(1)} %get-tuple-element.124), kind=kLoop, calls=%fused_computation.13 | loop fusion | flops 17301504 | bytes 52039936 | tf_op jit(solution)/shard_map/jit(_where)/select_n | solution.py:174
  262.0 71.7 %fusion.27 = f32[64,256,128]{1,2,0:T(8,128)} fusion(f32[64,1056,1,256]{3,2,1,0:T(1,128)} %param.7, f32[64,1056,64]{2,1,0:T(8,128)} %get-tuple-element.37, f32[64,1056,64]{2,1,0:T(8,128)} %get-tuple-element.36), kind=kOutput, calls=%fused_computation.50 | convolution fusion | flops 13296205824 | bytes 112197632 | tf_op jit(solution)/shard_map/srl,src->slc/dot_general | solution.py:179
  333.7 8.7 copy.51
  342.4 6.0 all-to-all-start
  348.4 2.2 fusion.95
  354.3 17.4 %collective-permute-start.1 = (f32[12,2,3,2048]{3,1,2,0:T(2,128)}, f32[12,2,3,2048]{3,1,2,0:T(2,128)}, u32[]{:S(2)}, u32[]{:S(2)}) collective-permute-start(f32[12,2,3,2048]{3,1,2,0:T(2,128)} %copy.87), channel_id=1, source_target_pairs={{1,0},{2,1},{3,2},{4,3},{5,4},{6,5},{7,6},{8,7},{9,8},{10,9},{11,1... | collective-permute-start | bytes 1769480 | tf_op jit(solution)/shard_map/ppermute | solution.py:37
  371.7 2.1 fusion.75
  383.7 144.9 %all-to-all-done = f32[64,256,128]{2,0,1:T(8,128)} async-done(((f32[64,256,128]{2,0,1:T(8,128)}), f32[64,256,128]{2,0,1:T(8,128)}, u32[]{:S(2)}, u32[]{:S(2)}) %all-to-all-start) | async-done | bytes 8388640 | tf_op jit(solution)/shard_map/all_to_all | solution.py:180
  528.6 12.2 %copy.53 = f32[8,64,32,128]{1,0,3,2:T(8,128)} copy(f32[8,64,32,128]{3,1,2,0:T(8,128)} %bitcast.23) | data formatting | bytes 16777216 | tf_op jit(solution)/shard_map/all_to_all | solution.py:180
  540.8 14.3 %reshape.327 = f32[512,32,2,2,32]{0,4,3,2,1:T(8,128)} reshape(f32[8,64,32,128]{1,0,3,2:T(8,128)} %copy.53) | data formatting | bytes 16777216 | tf_op jit(solution)/shard_map/reshape | solution.py:185
  555.1 4.7 slice_bitcast_fusion.1
  559.8 8.8 fusion.21
  568.6 11.1 bitcast_subtract_fusion
  583.1 1.9 collective-permute-start.2
  587.1 4.5 collective-permute-start.3
  591.7 2.5 collective-permute-done.3
  594.1 2.8 copy-done
  596.9 24.9 %shard_map.77 = (f32[12,2,32,2048]{3,2,1,0:T(8,128)}, f32[2,32,2048]{2,1,0:T(8,128)S(1)}) custom-call(s32[1]{0:T(128)} %bitcast.51.first_ref, f32[12,2]{1,0:T(8,128)S(1)} %copy.62.rate_ref, f32[12,2,32,2048]{3,2,1,0:T(8,128)S(1)} %copy-done, f32[12,2,3,2048]{3,2,1,0:T(4,128)S(1)} %copy.63.ql_ref, f32[12,2,3,2048]{3,2,1,0:T(4,128)S(1)} %copy.64.qh_ref, ...), custom_call_target="tpu_custom_call" | custom-call | tf_op jit(solution)/shard_map/pallas_call | solution.py:136
  626.3 10.0 fusion.37
  638.5 8.6 fusion.32
  647.6 4.6 pad_maximum_fusion.1
  652.2 10.3 copy.69
  662.5 14.2 %all-to-all-start.1 = ((f32[512,32,128]{2,1,0:T(8,128)}), f32[512,32,128]{2,1,0:T(8,128)}, u32[]{:S(2)}, u32[]{:S(2)}) async-start(f32[512,32,128]{2,1,0:T(8,128)} %copy.69), calls=%async_computation.1 | async-start | bytes 16777216 | tf_op jit(solution)/shard_map/all_to_all | solution.py:229
  677.0 178.8 %all-to-all-done.1 = f32[512,32,128]{2,1,0:T(8,128)} async-done(((f32[512,32,128]{2,1,0:T(8,128)}), f32[512,32,128]{2,1,0:T(8,128)}, u32[]{:S(2)}, u32[]{:S(2)}) %all-to-all-start.1) | async-done | bytes 8388640 | tf_op jit(solution)/shard_map/all_to_all | solution.py:229
  855.7 4.4 copy.70
  860.1 4.2 bitcast_multiply_fusion
  864.3 51.4 %fusion.10 = f32[1056,64,128]{2,0,1:T(8,128)} fusion(f32[64,256,128]{2,1,0:T(8,128)} %bitcast_multiply_fusion, f32[64,1056,1,256]{3,2,1,0:T(1,128)} %param.7), kind=kOutput, calls=%fused_computation.14 | convolution fusion | flops 13287555072 | bytes 112197632 | tf_op jit(solution)/shard_map/srl,slc->rsc/dot_general | solution.py:231
  915.7 36.9 %fusion.6 = f32[1056,64,64]{2,0,1:T(8,128)} fusion(f32[1056,64,128]{2,0,1:T(8,128)} %fusion.10, pred[1056,64]{0,1:T(8,128)(4,1)S(1)} %get-tuple-element.122, pred[1056,64]{0,1:T(8,128)(4,1)S(1)} %get-tuple-element.121), kind=kLoop, calls=%fused_computation.7 | loop fusion | flops 12976128 | bytes 52039680 | tf_op jit(solution)/shard_map/add | solution.py:233
  952.6 240.4 %reduce-scatter.2.cloned.1.call-done = f32[264,64,64]{2,0,1:T(8,128)} async-done(((f32[1056,64,64]{2,0,1:T(8,128)}), f32[264,64,64]{2,0,1:T(8,128)}) %reduce-scatter.2.cloned.1.call-update) | async-done | bytes 4325392 | tf_op jit(solution)/shard_map/reduce_scatter | solution.py:232
  1192.9 9.4 copy.71
  (97 shorter events, 28.5 us)
Async XLA Ops:
  7.2 219.9 %all-gather.2.cloned.1.call-start = ((), (), s32[]{:S(2)}) async-start(), calls=%async_computation.3 | async-start | bytes 43253760 | tf_op jit(solution)/shard_map/all_gather | solution.py:168
  16.0 0.7 copy-start.17
  16.8 0.6 copy-start.15
  16.8 0.6 copy-start.18
  16.9 0.6 copy-start.20
  17.5 0.6 copy-start.13
  342.4 186.2 %all-to-all-start = ((f32[64,256,128]{2,0,1:T(8,128)}), f32[64,256,128]{2,0,1:T(8,128)}, u32[]{:S(2)}, u32[]{:S(2)}) async-start(f32[64,256,128]{2,0,1:T(8,128)} %copy.51), calls=%async_computation | async-start | bytes 16777216 | tf_op jit(solution)/shard_map/all_to_all | solution.py:180
  351.1 234.1 %collective-permute-start = (f32[12,2,3,2048]{3,1,2,0:T(2,128)S(1)}, f32[12,2,3,2048]{3,1,2,0:T(2,128)S(1)}, u32[]{:S(2)}, u32[]{:S(2)}) collective-permute-start(f32[12,2,3,2048]{3,1,2,0:T(2,128)S(1)} %copy.86), channel_id=1, source_target_pairs={{0,1},{1,2},{2,3},{3,4},{4,5},{5,6},{6,7},{7,8},{8,9},{9,10},{10,1... | collective-permute-start | bytes 1769480 | tf_op jit(solution)/shard_map/ppermute | solution.py:34
  354.3 231.3 %collective-permute-start.1 = (f32[12,2,3,2048]{3,1,2,0:T(2,128)}, f32[12,2,3,2048]{3,1,2,0:T(2,128)}, u32[]{:S(2)}, u32[]{:S(2)}) collective-permute-start(f32[12,2,3,2048]{3,1,2,0:T(2,128)} %copy.87), channel_id=1, source_target_pairs={{1,0},{2,1},{3,2},{4,3},{5,4},{6,5},{7,6},{8,7},{9,8},{10,9},{11,1... | collective-permute-start | bytes 1769480 | tf_op jit(solution)/shard_map/ppermute | solution.py:37
  375.8 4.1 copy-start.7
  375.9 4.1 copy-start.10
  383.7 184.9 %copy-start.5 = (f32[512,1024]{1,0:T(8,128)}, f32[512,1024]{1,0:T(8,128)S(1)}, u32[]{:S(2)}) copy-start(f32[512,1024]{1,0:T(8,128)S(1)} %get-tuple-element.69) | copy-start | bytes 6291460
  555.1 4.7 copy-start.8
  555.1 4.7 copy-start.11
  579.7 2.0 copy-start.1
  579.7 3.4 copy-start.3
  579.7 5.3 copy-start.23
  583.1 8.5 collective-permute-start.2
  587.1 7.0 collective-permute-start.3
  594.1 2.8 copy-start
  596.9 24.9 %copy-start.2 = (f32[32,32,1024]{2,0,1:T(8,128)S(1)}, f32[32,32,1024]{2,0,1:T(8,128)}, u32[]{:S(2)}) copy-start(f32[32,32,1024]{2,0,1:T(8,128)} %copy-done.1) | copy-start | bytes 12582916
  596.9 24.9 %copy-start.4 = (f32[32,32,1024]{2,0,1:T(8,128)S(1)}, f32[32,32,1024]{2,0,1:T(8,128)}, u32[]{:S(2)}) copy-start(f32[32,32,1024]{2,0,1:T(8,128)} %copy-done.3) | copy-start | bytes 12582916
  624.7 1.6 copy-start.6
  636.3 1.6 copy-start.9
  636.3 2.2 copy-start.12
  662.5 14.2 %copy-start.14 = (pred[1056]{0:T(1024)(128)(4,1)S(1)}, pred[1056]{0:T(1024)(128)(4,1)}, u32[]{:S(2)}) copy-start(pred[1056]{0:T(1024)(128)(4,1)} %copy-done.13) | copy-start | bytes 3172
  662.5 14.2 %copy-start.16 = (pred[64]{0:T(512)(128)(4,1)S(1)}, pred[64]{0:T(512)(128)(4,1)}, u32[]{:S(2)}) copy-start(pred[64]{0:T(512)(128)(4,1)} %copy-done.15) | copy-start | bytes 196
  662.5 14.2 %copy-start.19 = (pred[64]{0:T(512)(128)(4,1)S(1)}, pred[64]{0:T(512)(128)(4,1)}, u32[]{:S(2)}) copy-start(pred[64]{0:T(512)(128)(4,1)} %copy-done.18) | copy-start | bytes 196
  662.5 14.2 %copy-start.21 = (s32[64]{0:T(128)S(1)}, s32[64]{0:T(128)}, u32[]{:S(2)}) copy-start(s32[64]{0:T(128)} %copy-done.20) | copy-start | bytes 772
  662.5 193.2 %all-to-all-start.1 = ((f32[512,32,128]{2,1,0:T(8,128)}), f32[512,32,128]{2,1,0:T(8,128)}, u32[]{:S(2)}, u32[]{:S(2)}) async-start(f32[512,32,128]{2,1,0:T(8,128)} %copy.69), calls=%async_computation.1 | async-start | bytes 16777216 | tf_op jit(solution)/shard_map/all_to_all | solution.py:229
  676.7 516.3 %reduce-scatter.2.cloned.1.call-start = ((), (), s32[]{:S(2)}) async-start(), calls=%async_computation.4 | async-start | bytes 43253760 | tf_op jit(solution)/shard_map/reduce_scatter | solution.py:232
  855.7 4.4 copy-start.22
Sparse Core Ops, SparseCore 0:
  16.2 210.8 all-gather.1
  952.7 240.1 reduce-scatter.1
where the time goes:
time: 1220 us; the launch traced here: 1210 us
  waiting for transfers between devices  775 us (64%)
  matrix products  162 us (13%)
  other arithmetic  97 us (8%)
  local copies, waits for them, and re-layouts  89.9 us (7%)
  starting transfers between devices  46 us (4%)
  Pallas kernels  24.9 us (2%)
  between operations  15 us (1%)
    reduce_scatter x1, waiting for transfers between devices, shards(): lax.psum_scatter(jnp.where(even_rows.T[:, :, None], row_sums[:, :, :colum...  240 us
    all_gather x1, waiting for transfers between devices, shards(): row_piece = lax.all_gather(coefs, 'pb', axis=1, tiled=True)  209 us
    all_to_all x1, waiting for transfers between devices, shards(): lax.all_to_all(fourier, 'ma', split_axis=0, concat_axis=1, tiled=True)  179 us
    all_to_all x1, waiting for transfers between devices, shards(): lax.all_to_all(legendre_sum, 'ma', split_axis=1, concat_axis=0, tiled=True)  145 us
    dot_general x1, matrix products, shards(): jnp.einsum('srl,src->slc', legendre_rows, masked, precision=HIGH)  71.7 us
    dot_general x1, matrix products, shards(): jnp.einsum('srl,slc->rsc', legendre_rows, weighted, precision=HIGH)  51.4 us
    add x1, other arithmetic, shards(): jnp.where(even_rows.T[:, :, None], row_sums[:, :, :columns], 0.0)  36.9 us
    select_n x1, other arithmetic, shards(): jnp.where(even_rows[:, :, None], row_piece * even_weight, 0.0)  34.9 us
  transfers between devices with their start and end apart: 8, of which 5 were waited for; matrix products, arithmetic and copies ran while one was open for 6% of the time, Pallas kernels for 0%

commit v1 on v0

--- a/solution.py
+++ b/solution.py
@@ -57,17 +57,6 @@
     cos = [cc[:, a : a + 1] * cf - sc[:, a : a + 1] * sf for a in range(points // step)]
     sin = [-(sc[:, a : a + 1] * cf + cc[:, a : a + 1] * sf) for a in range(points // step)]
     return jnp.stack([jnp.concatenate(cos, axis=1), jnp.concatenate(sin, axis=1)], axis=0)
-
-
-def row_masks(pair_ids, row_count):
-    row_ids = jnp.arange(row_count, dtype=jnp.int32)
-    bounds = (M - pair_ids)[:, None]
-    low_rows = row_ids[None, :] < bounds
-    high_rows = (row_ids[None, :] >= bounds) & (row_ids[None, :] <= M)
-    low_even = (pair_ids % 2 == 0)[:, None]
-    even_rows = (low_even & low_rows) | (~low_even & high_rows)
-    odd_rows = (low_even & high_rows) | (~low_even & low_rows)
-    return (even_rows, odd_rows)
 
 
 def transport_kernel(
@@ -154,42 +143,536 @@
     )
 
 
+MESH = pl.DeviceIdType.MESH
+GROUP = 8
+RING = 4
+
+
+def partner(index, count, step):
+    if step == 1:
+        return index + 1 - 2 * (index % 2)
+    if step == 2:
+        return (index + count // 2) % count
+    return count - 1 - index
+
+
+def split(x):
+    high = x.astype(jnp.bfloat16)
+    return high, (x - high.astype(jnp.float32)).astype(jnp.bfloat16)
+
+
+def product(left, right, contract):
+    dims = ((contract[:1], contract[1:]), ((), ()))
+    rows = left.shape[0]
+    left_high, left_low = split(left)
+    right_high, right_low = split(right)
+    both = lax.dot_general(
+        jnp.concatenate([left_high, left_low], axis=0), right_high, dims,
+        preferred_element_type=jnp.float32,
+    )
+    rest = lax.dot_general(left_high, right_low, dims, preferred_element_type=jnp.float32)
+    return both[:rows] + (both[rows:] + rest)
+
+
+def rows_of(ref, start, count):
+    return jnp.concatenate(
+        [ref[pl.ds(2 * start, count, 2), :], ref[pl.ds(2 * start + 1, count, 2), :]], axis=1
+    )
+
+
+def order_rows(pair_ref, slot, first, count):
+    pair = pair_ref[slot]
+    bound = M - pair
+    low_even = pair % 2 == 0
+    even_from, even_to = jnp.where(low_even, 0, bound), jnp.where(low_even, bound, M + 1)
+    odd_from, odd_to = jnp.where(low_even, bound, 0), jnp.where(low_even, M + 1, bound)
+    rows = first + lax.broadcasted_iota(jnp.int32, (1, count), 1)
+    even = (rows >= even_from) & (rows < even_to)
+    odd = (rows >= odd_from) & (rows < odd_to)
+    return even, odd, jnp.where(pair == 0, 1.0, 2.0)
+
+
+def enter(band_count, here, quarter_count, quarter):
+    barrier = pltpu.get_barrier_semaphore()
+    for step in range(1, band_count):
+        pl.semaphore_signal(
+            barrier, inc=1, device_id={"ma": (here + step) % band_count}, device_id_type=MESH
+        )
+    for step in (1, 2):
+        pl.semaphore_signal(
+            barrier, inc=1, device_id={"pb": partner(quarter, quarter_count, step)},
+            device_id_type=MESH,
+        )
+    pl.semaphore_wait(barrier, band_count + 1)
+
+
+def stream_rows(legendre_ref, held, sem, slot):
+    return pltpu.make_async_copy(legendre_ref.at[slot], held.at[slot % RING], sem.at[slot % RING])
+
+
+def analysis_kernel(
+    pair_ref, coefs_ref, legendre_ref, out_ref,
+    pieces, held, sums, load_sem, own_sem, near_send, near_recv, far_send, far_recv,
+    pass_send, pass_recv, send_sem, recv_sem, keep_sem,
+):
+    slots, columns, piece = coefs_ref.shape
+    chunks = slots // GROUP
+    count = lax.axis_size("ma")
+    here = lax.axis_index("ma")
+    quarters = lax.axis_size("pb")
+    quarter = lax.axis_index("pb")
+    near, far = partner(quarter, quarters, 1), partner(quarter, quarters, 2)
+    band = sums.shape[1] // count
+    width = sums.shape[1] // GROUP
+    weight_columns = 2 * columns
+
+    def part(ref, chunk):
+        return ref.at[pl.ds(chunk * GROUP, GROUP)]
+
+    def own(chunk):
+        return pltpu.make_async_copy(
+            part(coefs_ref, chunk), part(pieces.at[0], chunk), own_sem.at[chunk]
+        )
+
+    def to_near(chunk):
+        return pltpu.make_async_remote_copy(
+            part(coefs_ref, chunk), part(pieces.at[1], chunk),
+            near_send.at[chunk], near_recv.at[chunk],
+            device_id={"pb": near}, device_id_type=MESH,
+        )
+
+    def to_far(chunk):
+        return pltpu.make_async_remote_copy(
+            part(coefs_ref, chunk), part(pieces.at[2], chunk),
+            far_send.at[chunk], far_recv.at[chunk],
+            device_id={"pb": far}, device_id_type=MESH,
+        )
+
+    def pass_on(chunk):
+        return pltpu.make_async_remote_copy(
+            part(pieces.at[2], chunk), part(pieces.at[3], chunk),
+            pass_send.at[chunk], pass_recv.at[chunk],
+            device_id={"pb": near}, device_id_type=MESH,
+        )
+
+    def to_band(chunk, step):
+        target = (here + step) % count
+        return pltpu.make_async_remote_copy(
+            sums.at[chunk, pl.ds(target * band, band)], out_ref.at[here, chunk],
+            send_sem.at[step - 1, chunk], recv_sem.at[step - 1, chunk],
+            device_id={"ma": target}, device_id_type=MESH,
+        )
+
+    def keep(chunk):
+        return pltpu.make_async_copy(
+            sums.at[chunk, pl.ds(here * band, band)], out_ref.at[here, chunk], keep_sem.at[chunk]
+        )
+
+    for slot in range(RING - 1):
+        stream_rows(legendre_ref, held, load_sem, slot).start()
+    enter(count, here, quarters, quarter)
+
+    def begin(chunk, carry):
+        to_far(chunk).start()
+        to_near(chunk).start()
+        own(chunk).start()
+        return carry
+
+    lax.fori_loop(0, chunks, begin, 0)
+
+    def one_slot(slot, chunk):
+        stream_rows(legendre_ref, held, load_sem, slot).wait()
+
+        @pl.when(slot + RING - 1 < slots)
+        def _():
+            stream_rows(legendre_ref, held, load_sem, slot + RING - 1).start()
+
+        block = held.at[slot % RING]
+        total = jnp.zeros((weight_columns, width), jnp.float32)
+        for k in range(quarters):
+            first = (quarter if k == 0 else partner(quarter, quarters, k)) * piece
+            even, odd, even_weight = order_rows(pair_ref, slot, first, piece)
+            x = pieces[k, slot]
+            both = jnp.concatenate(
+                [jnp.where(even, x * even_weight, 0.0), jnp.where(odd, x * 2.0, 0.0)], axis=0
+            )
+            total = total + product(both, rows_of(block, first, piece), (1, 0))
+        sums[chunk, pl.ds(slot % GROUP, width, GROUP), :] = total.T
+
+    def one_chunk(chunk, carry):
+        to_far(chunk).wait_recv()
+        pass_on(chunk).start()
+        own(chunk).wait()
+        to_near(chunk).wait_recv()
+        pass_on(chunk).wait_recv()
+
+        def body(i, inner):
+            one_slot(chunk * GROUP + i, chunk)
+            return inner
+
+        lax.fori_loop(0, GROUP, body, 0)
+        keep(chunk).start()
+        for step in range(1, count):
+            to_band(chunk, step).start()
+        return carry
+
+    lax.fori_loop(0, chunks, one_chunk, 0)
+
+    def finish(chunk, carry):
+        to_far(chunk).wait_send()
+        to_near(chunk).wait_send()
+        pass_on(chunk).wait_send()
+        keep(chunk).wait()
+        for step in range(1, count):
+            to_band(chunk, step).wait()
+        return carry
+
+    lax.fori_loop(0, chunks, finish, 0)
+
+
+def analysis(pairs, coefs, legendre, band_count):
+    slots, columns, piece = coefs.shape
+    chunks = slots // GROUP
+    half_rows, lanes = legendre.shape[1:]
+    quarters = half_rows // (2 * piece)
+    width = 2 * lanes
+    band = width // band_count
+    any_space = pl.BlockSpec(memory_space=pl.ANY)
+    dma = pltpu.SemaphoreType.DMA
+    return pl.pallas_call(
+        analysis_kernel,
+        in_specs=[pl.BlockSpec(memory_space=pltpu.SMEM), any_space, any_space],
+        out_specs=any_space,
+        out_shape=jax.ShapeDtypeStruct(
+            (band_count, chunks, band * GROUP, 2 * columns), jnp.float32
+        ),
+        scratch_shapes=[
+            pltpu.VMEM((quarters, slots, columns, piece), jnp.float32),
+            pltpu.VMEM((RING, half_rows, lanes), jnp.float32),
+            pltpu.VMEM((chunks, width * GROUP, 2 * columns), jnp.float32),
+            dma((RING,)),
+        ]
+        + [dma((chunks,))] * 7
+        + [dma((band_count - 1, chunks))] * 2
+        + [dma((chunks,))],
+        compiler_params=pltpu.CompilerParams(
+            collective_id=0, has_side_effects=True, vmem_limit_bytes=60 * 1024 * 1024
+        ),
+    )(pairs, coefs, legendre)
+
+
+def synthesis_kernel(
+    pair_ref, quad_ref, fourier_ref, legendre_ref, out_ref,
+    bands, held, parts, near_held, far_held, load_sem, send_sem, recv_sem, keep_sem,
+    near_send, near_recv, far_send, far_recv, out_sem,
+):
+    slots, columns, piece = out_ref.shape
+    chunks = slots // GROUP
+    count = lax.axis_size("ma")
+    here = lax.axis_index("ma")
+    quarters = lax.axis_size("pb")
+    quarter = lax.axis_index("pb")
+    near, far = partner(quarter, quarters, 1), partner(quarter, quarters, 2)
+    band = bands.shape[1] // count
+    width = bands.shape[1] // GROUP
+
+    def to_orders(chunk, step):
+        target = (here + step) % count
+        return pltpu.make_async_remote_copy(
+            fourier_ref.at[target, chunk], bands.at[chunk, pl.ds(here * band, band)],
+            send_sem.at[step - 1, chunk], recv_sem.at[step - 1, chunk],
+            device_id={"ma": target}, device_id_type=MESH,
+        )
+
+    def keep(chunk):
+        return pltpu.make_async_copy(
+            fourier_ref.at[here, chunk], bands.at[chunk, pl.ds(here * band, band)],
+            keep_sem.at[chunk],
+        )
+
+    def to_near(chunk, k):
+        return pltpu.make_async_remote_copy(
+            parts.at[chunk, 2 * k + 1], near_held.at[chunk, k],
+            near_send.at[k, chunk], near_recv.at[k, chunk],
+            device_id={"pb": near}, device_id_type=MESH,
+        )
+
+    def to_far(chunk):
+        return pltpu.make_async_remote_copy(
+            parts.at[chunk, 2], far_held.at[chunk], far_send.at[chunk], far_recv.at[chunk],
+            device_id={"pb": far}, device_id_type=MESH,
+        )
+
+    def store(chunk):
+        return pltpu.make_async_copy(
+            parts.at[chunk, 0], out_ref.at[pl.ds(chunk * GROUP, GROUP)], out_sem.at[chunk]
+        )
+
+    for slot in range(RING - 1):
+        stream_rows(legendre_ref, held, load_sem, slot).start()
+    enter(count, here, quarters, quarter)
+
+    def begin(chunk, carry):
+        for step in range(1, count):
+            to_orders(chunk, step).start()
+        keep(chunk).start()
+        return carry
+
+    lax.fori_loop(0, chunks, begin, 0)
+
+    def one_slot(slot, chunk):
+        stream_rows(legendre_ref, held, load_sem, slot).wait()
+
+        @pl.when(slot + RING - 1 < slots)
+        def _():
+            stream_rows(legendre_ref, held, load_sem, slot + RING - 1).start()
+
+        block = held.at[slot % RING]
+        own = slot % GROUP
+        weighted = bands[chunk, pl.ds(own, width, GROUP), :].T * quad_ref[...]
+        for k in range(quarters):
+            first = (quarter if k == 0 else partner(quarter, quarters, k)) * piece
+            even, odd, _ = order_rows(pair_ref, slot, first, piece)
+            both = product(weighted, rows_of(block, first, piece), (1, 1))
+            parts[chunk, k, own] = jnp.where(
+                even, both[:columns], jnp.where(odd, both[columns:], 0.0)
+            )
+
+    def complete(chunk):
+        to_far(chunk).wait_recv()
+
+        def body(i, carry):
+            parts[chunk, 0, i] = parts[chunk, 0, i] + near_held[chunk, 0, i] + far_held[chunk, i]
+            return carry
+
+        lax.fori_loop(0, GROUP, body, 0)
+        store(chunk).start()
+
+    def one_chunk(chunk, carry):
+        keep(chunk).wait()
+        for step in range(1, count):
+            to_orders(chunk, step).wait_recv()
+
+        def body(i, inner):
+            one_slot(chunk * GROUP + i, chunk)
+            return inner
+
+        lax.fori_loop(0, GROUP, body, 0)
+        to_near(chunk, 1).start()
+        to_near(chunk, 0).start()
+
+        @pl.when(chunk > 0)
+        def _():
+            complete(chunk - 1)
+
+        to_near(chunk, 1).wait_recv()
+
+        def add(i, inner):
+            parts[chunk, 2, i] = parts[chunk, 2, i] + near_held[chunk, 1, i]
+            return inner
+
+        lax.fori_loop(0, GROUP, add, 0)
+        to_near(chunk, 0).wait_recv()
+        to_far(chunk).start()
+        return carry
+
+    lax.fori_loop(0, chunks, one_chunk, 0)
+    complete(chunks - 1)
+
+    def finish(chunk, carry):
+        for step in range(1, count):
+            to_orders(chunk, step).wait_send()
+        to_near(chunk, 0).wait_send()
+        to_near(chunk, 1).wait_send()
+        to_far(chunk).wait_send()
+        store(chunk).wait()
+        return carry
+
+    lax.fori_loop(0, chunks, finish, 0)
+
+
+def synthesis(pairs, quad, fourier, legendre, piece):
+    band_count, chunks, rows, columns = fourier.shape
+    slots = chunks * GROUP
+    columns = columns // 2
+    half_rows, lanes = legendre.shape[1:]
+    quarters = half_rows // (2 * piece)
+    any_space = pl.BlockSpec(memory_space=pl.ANY)
+    dma = pltpu.SemaphoreType.DMA
+    block = (GROUP, columns, piece)
+    return pl.pallas_call(
+        synthesis_kernel,
+        in_specs=[
+            pl.BlockSpec(memory_space=pltpu.SMEM), pl.BlockSpec(memory_space=pltpu.VMEM),
+            any_space, any_space,
+        ],
+        out_specs=any_space,
+        out_shape=jax.ShapeDtypeStruct((slots, columns, piece), jnp.float32),
+        scratch_shapes=[
+            pltpu.VMEM((chunks, band_count * rows, 2 * columns), jnp.float32),
+            pltpu.VMEM((RING, half_rows, lanes), jnp.float32),
+            pltpu.VMEM((chunks, quarters) + block, jnp.float32),
+            pltpu.VMEM((chunks, 2) + block, jnp.float32),
+            pltpu.VMEM((chunks,) + block, jnp.float32),
+            dma((RING,)),
+            dma((band_count - 1, chunks)),
+            dma((band_count - 1, chunks)),
+            dma((chunks,)),
+            dma((2, chunks)),
+            dma((2, chunks)),
+            dma((chunks,)),
+            dma((chunks,)),
+            dma((chunks,)),
+        ],
+        compiler_params=pltpu.CompilerParams(
+            collective_id=1, has_side_effects=True, vmem_limit_bytes=63 * 1024 * 1024
+        ),
+    )(pairs, quad, fourier, legendre)
+
+
+LATS = 8
+
+
+def to_grid_kernel(spectral_ref, high_ref, low_ref, out_ref, left):
+    sources, chunks = spectral_ref.shape[:2]
+    slots = sources * chunks * GROUP
+    part = NF * LAYER_TOTAL
+    half = high_ref.shape[2]
+
+    for j in range(LATS):
+        block = spectral_ref[:, :, j * GROUP : (j + 1) * GROUP, :].reshape(slots, 4 * part).T
+        for h in range(2):
+            for p in range(2):
+                left[h, j * part : (j + 1) * part, p * slots : (p + 1) * slots] = block[
+                    (2 * h + p) * part : (2 * h + p + 1) * part
+                ]
+    sums = []
+    for h in range(2):
+        high, low = split(left[h])
+        dot = lambda a, b: jnp.dot(a, b, preferred_element_type=jnp.float32)
+        sums.append(dot(high, high_ref[h]) + (dot(low, high_ref[h]) + dot(high, low_ref[h])))
+    out_ref[:, :half] = sums[0] + sums[1]
+    out_ref[:, half:] = sums[0] - sums[1]
+
+
+def to_grid(spectral, high, low):
+    sources, chunks, rows, lanes = spectral.shape
+    part = NF * LAYER_TOTAL
+    lats = rows // GROUP
+    tables = pl.BlockSpec(high.shape, lambda j: (0, 0, 0))
+    return pl.pallas_call(
+        to_grid_kernel,
+        grid=(lats // LATS,),
+        in_specs=[
+            pl.BlockSpec((sources, chunks, LATS * GROUP, lanes), lambda j: (0, 0, j, 0)),
+            tables,
+            tables,
+        ],
+        out_specs=pl.BlockSpec((LATS * part, NLON), lambda j: (j, 0)),
+        out_shape=jax.ShapeDtypeStruct((lats * part, NLON), jnp.float32),
+        scratch_shapes=[pltpu.VMEM((2, LATS * part, high.shape[1]), jnp.float32)],
+        compiler_params=pltpu.CompilerParams(vmem_limit_bytes=60 * 1024 * 1024),
+    )(spectral, high, low)
+
+
+def from_grid_kernel(field_ref, heat_ref, high_ref, low_ref, out_ref, left, turned):
+    sources, chunks = out_ref.shape[:2]
+    slots = sources * chunks * GROUP
+    part = NF * LAYER_TOTAL
+    half = high_ref.shape[2]
+    lev = LAYER_TOTAL
+
+    for j in range(LATS):
+        def tendency(cols):
+            at = lambda f: field_ref[j * part + f * lev : j * part + (f + 1) * lev, cols]
+            u, v, t, q = at(0), at(1), at(2), at(3)
+            speed = jnp.sqrt(u * u + v * v + 1.0)
+            moist = MOISTURE_SOURCE * t * q
+            return jnp.concatenate(
+                [
+                    -DRAG_COEFFICIENT * speed * u,
+                    -DRAG_COEFFICIENT * speed * v,
+                    heat_ref[j, :, cols] - moist,
+                    moist - RAINFALL_FACTOR * speed * q,
+                ],
+                axis=0,
+            )
+
+        near = tendency(slice(0, half))
+        far = tendency(slice(half, 2 * half))
+        left[0, j * part : (j + 1) * part] = near + far
+        left[1, j * part : (j + 1) * part] = near - far
+    dims = (((1,), (1,)), ((), ()))
+    for h in range(2):
+        high, low = split(left[h])
+        dot = lambda a, b: lax.dot_general(a, b, dims, preferred_element_type=jnp.float32)
+        both = dot(high, high_ref[h]) + (dot(low, high_ref[h]) + dot(high, low_ref[h]))
+        for j in range(LATS):
+            for p in range(2):
+                turned[j, (2 * h + p) * part : (2 * h + p + 1) * part] = both[
+                    j * part : (j + 1) * part, p * slots : (p + 1) * slots
+                ]
+    for j in range(LATS):
+        out_ref[:, :, j * GROUP : (j + 1) * GROUP, :] = turned[j].T.reshape(
+            sources, chunks, GROUP, 4 * part
+        )
+
+
+def from_grid(field, heat, high, low, sources, chunks):
+    part = NF * LAYER_TOTAL
+    lats = field.shape[0] // part
+    slots = sources * chunks * GROUP
+    tables = pl.BlockSpec(high.shape, lambda j: (0, 0, 0))
+    return pl.pallas_call(
+        from_grid_kernel,
+        grid=(lats // LATS,),
+        in_specs=[
+            pl.BlockSpec((LATS * part, NLON), lambda j: (j, 0)),
+            pl.BlockSpec((LATS, LAYER_TOTAL, NLON), lambda j: (j, 0, 0)),
+            tables,
+            tables,
+        ],
+        out_specs=pl.BlockSpec(
+            (sources, chunks, LATS * GROUP, 4 * part), lambda j: (0, 0, j, 0)
+        ),
+        out_shape=jax.ShapeDtypeStruct((sources, chunks, lats * GROUP, 4 * part), jnp.float32),
+        scratch_shapes=[
+            pltpu.VMEM((2, LATS * part, high.shape[2]), jnp.float32),
+            pltpu.VMEM((LATS, 4 * part, slots), jnp.float32),
+        ],
+        compiler_params=pltpu.CompilerParams(vmem_limit_bytes=60 * 1024 * 1024),
+    )(field, heat, high, low)
+
+
+def fourier_tables(pair_of_slot):
+    _, even_all, odd_all = split_orders(pair_of_slot)
+    half = NLON // 2
+    tables = jnp.stack([half_tables(even_all, half), half_tables(odd_all, half)], axis=0)
+    tables = tables.reshape(2, -1, half)
+    high = lax.reduce_precision(tables, 8, 7)
+    return high.astype(jnp.bfloat16), (tables - high).astype(jnp.bfloat16)
+
+
 def shards(coefs, legendre, quad_weight, pair_of_slot, tracers, heat_rate):
-    slot_count = coefs.shape[0]
-    columns = coefs.shape[2]
+    slot_count, piece = coefs.shape[:2]
     quarter = legendre.shape[3]
-    half = NLON // 2
     part = NF * LAYER_TOTAL
-    legendre_rows = legendre.reshape(slot_count, legendre.shape[1], quarter)
+    band_count = lax.axis_size("ma")
+    lanes = 128
+    legendre_rows = legendre.reshape(slot_count, -1, lanes)
     own_pairs = lax.dynamic_slice_in_dim(
         pair_of_slot, lax.axis_index("ma") * slot_count, slot_count, 0
     )
     low, high = halo_rows(tracers, ("ma", "pb"), 2, HALO)
-    row_piece = lax.all_gather(coefs, "pb", axis=1, tiled=True)
-    even_rows, odd_rows = row_masks(own_pairs, row_piece.shape[1])
-    even_orders = split_orders(own_pairs)[1]
-    even_weight = jnp.where(even_orders == 0, 1.0, 2.0).astype(jnp.float32)[:, None, None]
-    masked = jnp.concatenate(
-        [
-            jnp.where(even_rows[:, :, None], row_piece * even_weight, 0.0),
-            jnp.where(odd_rows[:, :, None], row_piece * 2.0, 0.0),
-        ],
-        axis=2,
-    )
-    legendre_sum = jnp.einsum("srl,src->slc", legendre_rows, masked, precision=HIGH)
-    bands = lax.all_to_all(legendre_sum, "ma", split_axis=1, concat_axis=0, tiled=True)
-    band_rows = bands.shape[1]
-    _, even_all, odd_all = split_orders(pair_of_slot)
-    even_table = half_tables(even_all, half)
-    odd_table = half_tables(odd_all, half)
-    spectral = bands.reshape(PAIRS, band_rows, 2, 2, part)
-    even_sum = jnp.einsum("sjpc,psi->jci", spectral[:, :, 0], even_table, precision=HIGH)
-    odd_sum = jnp.einsum("sjpc,psi->jci", spectral[:, :, 1], odd_table, precision=HIGH)
-    field = jnp.concatenate([even_sum + odd_sum, even_sum - odd_sum], axis=2)
+    table_high, table_low = fourier_tables(pair_of_slot)
+    spectral = analysis(own_pairs, jnp.transpose(coefs, (0, 2, 1)), legendre_rows, band_count)
+    field = to_grid(spectral, table_high, table_low)
+    band_rows = field.shape[0] // part
+    grid = field.reshape(band_rows, part, NLON)
     wind = jnp.stack(
         [
-            jnp.transpose(field[:, 0:TLEV, :], (1, 0, 2)),
-            jnp.transpose(field[:, LAYER_TOTAL : LAYER_TOTAL + TLEV, :], (1, 0, 2)),
+            jnp.transpose(grid[:, 0:TLEV, :], (1, 0, 2)),
+            jnp.transpose(grid[:, LAYER_TOTAL : LAYER_TOTAL + TLEV, :], (1, 0, 2)),
         ],
         axis=0,
     )
@@ -199,44 +682,12 @@
         first_row, heat_rate, tracers, low, high, wind, wind_low, wind_high
     )
     heating = jnp.transpose(heating, (1, 0, 2))
-    u = field[:, 0:LAYER_TOTAL]
-    v = field[:, LAYER_TOTAL : 2 * LAYER_TOTAL]
-    t = field[:, 2 * LAYER_TOTAL : 3 * LAYER_TOTAL]
-    q = field[:, 3 * LAYER_TOTAL : 4 * LAYER_TOTAL]
-    speed = jnp.sqrt(u * u + v * v + 1.0)
     warming = jnp.pad(heating, ((0, 0), (0, LAYER_TOTAL - TLEV), (0, 0)))
-    moist = MOISTURE_SOURCE * t * q
-    tendency = jnp.concatenate(
-        [
-            -DRAG_COEFFICIENT * speed * u,
-            -DRAG_COEFFICIENT * speed * v,
-            warming - moist,
-            moist - RAINFALL_FACTOR * speed * q,
-        ],
-        axis=1,
-    )
-    near = tendency[:, :, :half]
-    far = tendency[:, :, half:]
-    even_fourier = jnp.einsum("jci,psi->sjpc", near + far, even_table, precision=HIGH)
-    odd_fourier = jnp.einsum("jci,psi->sjpc", near - far, odd_table, precision=HIGH)
-    fourier = jnp.concatenate(
-        [
-            even_fourier.reshape(PAIRS, band_rows, columns),
-            odd_fourier.reshape(PAIRS, band_rows, columns),
-        ],
-        axis=2,
-    )
-    by_orders = lax.all_to_all(fourier, "ma", split_axis=0, concat_axis=1, tiled=True)
-    weighted = by_orders * quad_weight.reshape(quarter)[None, :, None]
-    row_sums = jnp.einsum("srl,slc->rsc", legendre_rows, weighted, precision=HIGH)
-    summed = lax.psum_scatter(
-        jnp.where(even_rows.T[:, :, None], row_sums[:, :, :columns], 0.0)
-        + jnp.where(odd_rows.T[:, :, None], row_sums[:, :, columns:], 0.0),
-        "pb",
-        scatter_dimension=0,
-        tiled=True,
-    )
-    return (jnp.transpose(summed, (1, 0, 2)), new_tracers)
+    fourier = from_grid(
+        field, warming, table_high, table_low, band_count, slot_count // GROUP
+    )
+    spec = synthesis(own_pairs, quad_weight.reshape(1, quarter), fourier, legendre_rows, piece)
+    return (jnp.transpose(spec, (0, 2, 1)), new_tracers)
 
 
 def solution(mesh):

time: 1220 us -> 580 us (0.48)
  waiting for transfers between devices: 775 us -> 8.76 us
  Pallas kernels: 24.9 us -> 525 us
  matrix products: 162 us -> 0 us
  other arithmetic: 97 us -> 11.9 us
  local copies, waits for them, and re-layouts: 89.9 us -> 21.3 us
  starting transfers between devices: 46 us -> 10.5 us
  between operations: 15 us -> 0.96 us
    pallas_call x0 -> x4, Pallas kernels: none -> 500 us  [the longest x1 243 us: synthesis(): pl.pallas_call(synthesis_kernel, in_specs=[pl.BlockSpec(memory_space=pltp...]
    all_to_all x2 -> x0, waiting for transfers between devices: 324 us -> none  [the longest x1 179 us: shards(): lax.all_to_all(fourier, 'ma', split_axis=0, concat_axis=1, tiled=True)]
    reduce_scatter x1 -> x0, waiting for transfers between devices: 240 us -> none  [shards(): lax.psum_scatter(jnp.where(even_rows.T[:, :, None], row_sums[:, :, :colum...]
    all_gather x1 -> x0, waiting for transfers between devices: 209 us -> none  [shards(): row_piece = lax.all_gather(coefs, 'pb', axis=1, tiled=True)]
    dot_general x6 -> x0, matrix products: 162 us -> none  [the longest x1 71.7 us: shards(): jnp.einsum('srl,src->slc', legendre_rows, masked, precision=HIGH)]
    add x2 -> x0, other arithmetic: 38 us -> none  [the longest x1 36.9 us: shards(): jnp.where(even_rows.T[:, :, None], row_sums[:, :, :columns], 0.0)]
    select_n x2 -> x0, other arithmetic: 35 us -> none  [the longest x1 34.9 us: shards(): jnp.where(even_rows[:, :, None], row_piece * even_weight, 0.0)]
    all_to_all x2 -> x0, starting transfers between devices: 20.2 us -> none  [the longest x1 14.2 us: shards(): lax.all_to_all(fourier, 'ma', split_axis=0, concat_axis=1, tiled=True)]
  transfers between devices with their start and end apart: 8 -> 4, of which waited for: 5 -> 1; matrix products, arithmetic and copies ran while one was open for 6% -> 1% of each run, Pallas kernels for 0% -> 0%
where the time goes in v1:
time: 580 us; the launch traced here: 579 us
  Pallas kernels  525 us (91%)
  local copies, waits for them, and re-layouts  21.3 us (4%)
  other arithmetic  11.9 us (2%)
  starting transfers between devices  10.5 us (2%)
  waiting for transfers between devices  8.76 us (2%)
    pallas_call x1, Pallas kernels, synthesis(): pl.pallas_call(synthesis_kernel, in_specs=[pl.BlockSpec(memory_space=pltp...  243 us
    pallas_call x1, Pallas kernels, analysis(): pl.pallas_call(analysis_kernel, in_specs=[pl.BlockSpec(memory_space=pltpu...  213 us
    pallas_call x1, Pallas kernels, transport(): pl.pallas_call(transport_kernel, grid=(levels, count), in_specs=[smem, sm...  24.9 us
    pallas_call x1, Pallas kernels, from_grid(): pl.pallas_call(from_grid_kernel, grid=(lats // LATS,), in_specs=[pl.Block...  22.3 us
    pallas_call x1, Pallas kernels, to_grid(): pl.pallas_call(to_grid_kernel, grid=(lats // LATS,), in_specs=[pl.BlockSp...  21.5 us
  transfers between devices with their start and end apart: 4, of which 1 were waited for; matrix products, arithmetic and copies ran while one was open for 1% of the time, Pallas kernels for 0%

profile of v1, /device:TPU:12, one launch (start us, length us, event | category | flops | bytes accessed | tf_op | source)
XLA Modules:
  0.0 578.6 jit_solution(5302598803730749576)
XLA Ops:
  0.6 0.7 broadcast_subtract_fusion
  1.3 1.3 dynamic_slice.3.pair_ref
  2.6 2.1 fusion.13
  4.7 0.2 sine_multiply_fusion.1
  6.7 0.3 pad_maximum_fusion.1
  8.7 0.3 pad_maximum_fusion.2
  9.1 4.3 fusion
  13.3 213.1 %shard_map.77.spectral_ref = f32[8,8,256,128]{3,2,1,0:T(8,128)} custom-call(s32[64]{0:T(128)} %dynamic_slice.3.pair_ref, f32[64,64,264]{2,1,0:T(8,128)} %bitcast.74, f32[64,2112,128]{2,1,0:T(8,128)} %bitcast.1.legendre_ref), custom_call_target="tpu_custom_call" | custom-call | tf_op jit(solution)/shard_map/pallas_call | solution.py:342
  226.5 21.5 %shard_map.78.field_ref = f32[1024,2048]{1,0:T(8,128)} custom-call(f32[8,8,256,128]{3,2,1,0:T(8,128)} %shard_map.77.spectral_ref, bf16[2,1024,1024]{2,1,0:T(8,128)(2,1)} %get-tuple-element.27.high_ref, bf16[2,1024,1024]{2,1,0:T(8,128)(2,1)} %get-tuple-element.26.low_ref), custom_call_target="tpu_custom_call" | custom-call | tf_op jit(solution)/shard_map/pallas_call | solution.py:563
  248.0 2.5 fusion.25
  250.6 0.3 copy.32
  250.9 0.3 copy.33
  251.2 0.7 pad_maximum_fusion.3
  251.9 2.1 collective-permute-start.3
  254.0 2.2 fusion.26
  256.2 0.5 copy.22
  256.7 2.4 collective-permute-start
  259.1 0.5 copy.23
  259.6 4.1 collective-permute-start.1
  263.6 1.9 collective-permute-start.2
  265.7 0.9 slice_bitcast_fusion
  266.6 8.7 %collective-permute-done.2 = f32[2,2,3,2048]{3,2,1,0:T(4,128)} collective-permute-done((f32[2,2,3,2048]{3,2,1,0:T(4,128)S(1)}, f32[2,2,3,2048]{3,2,1,0:T(4,128)}, u32[]{:S(2)}, u32[]{:S(2)}) %collective-permute-start.2) | collective-permute-done | bytes 98336 | tf_op jit(solution)/shard_map/ppermute | solution.py:34
  275.3 0.9 slice_bitcast_fusion.1
  276.2 0.4 copy.19.ql_ref
  276.7 0.4 copy.20.qh_ref
  277.1 2.8 copy-done
  279.9 24.9 %shard_map.79 = (f32[12,2,32,2048]{3,2,1,0:T(8,128)}, f32[2,32,2048]{2,1,0:T(8,128)S(1)}) custom-call(s32[1]{0:T(128)} %bitcast.40.first_ref, f32[12,2]{1,0:T(8,128)S(1)} %copy.18.rate_ref, f32[12,2,32,2048]{3,2,1,0:T(8,128)S(1)} %copy-done, f32[12,2,3,2048]{3,2,1,0:T(4,128)S(1)} %copy.19.ql_ref, f32[12,2,3,2048]{3,2,1,0:T(4,128)S(1)} %copy.20.qh_ref, ...), custom_call_target="tpu_custom_call" | custom-call | tf_op jit(solution)/shard_map/pallas_call | solution.py:125
  304.8 0.4 copy.31
  305.2 1.6 pad.4.heat_ref
  306.8 22.3 %shard_map.80.fourier_ref = f32[8,8,256,128]{3,2,1,0:T(8,128)} custom-call(f32[1024,2048]{1,0:T(8,128)} %shard_map.78.field_ref, f32[32,8,2048]{2,1,0:T(8,128)} %pad.4.heat_ref, bf16[2,1024,1024]{2,1,0:T(8,128)(2,1)} %get-tuple-element.27.high_ref, bf16[2,1024,1024]{2,1,0:T(8,128)(2,1)} %get-tuple-element.26.low_ref), custom_call_target="tpu_custom_call" | custom-call | tf_op jit(solution)/shard_map/pallas_call | solution.py:626
  329.1 243.3 %shard_map.81 = f32[64,64,264]{2,1,0:T(8,128)} custom-call(s32[64]{0:T(128)} %dynamic_slice.3.pair_ref, f32[1,256]{1,0:T(1,128)} %quad_ref.1, f32[8,8,256,128]{3,2,1,0:T(8,128)} %shard_map.80.fourier_ref, f32[64,2112,128]{2,1,0:T(8,128)} %bitcast.1.legendre_ref), custom_call_target="tpu_custom_call" | custom-call | tf_op jit(solution)/shard_map/pallas_call | solution.py:503
  572.4 6.2 %copy.63 = f32[64,264,64]{1,2,0:T(8,128)} copy(f32[64,264,64]{1,2,0:T(8,128)} %bitcast.71) | data formatting | bytes 8650752
  (26 shorter events, 3.4 us)
Async XLA Ops:
  251.9 13.8 %collective-permute-start.3 = (f32[2,2,3,2048]{3,2,1,0:T(4,128)}, f32[2,2,3,2048]{3,2,1,0:T(4,128)}, u32[]{:S(2)}, u32[]{:S(2)}) collective-permute-start(f32[2,2,3,2048]{3,2,1,0:T(4,128)} %get-tuple-element.30), channel_id=1, source_target_pairs={{1,0},{2,1},{3,2},{4,3},{5,4},{6,5},{7,6},{8,7},{9,8},{10,9},{11,1... | collective-permute-start | bytes 294920 | tf_op jit(solution)/shard_map/ppermute | solution.py:37
  256.2 9.4 %copy-start.1 = (f32[12,2]{0,1:T(2,128)S(1)}, f32[12,2]{0,1:T(2,128)}, u32[]{:S(2)}) copy-start(f32[12,2]{0,1:T(2,128)} %param.11) | copy-start | bytes 292
  256.7 19.5 %collective-permute-start = (f32[12,2,3,2048]{3,1,2,0:T(2,128)S(1)}, f32[12,2,3,2048]{3,1,2,0:T(2,128)S(1)}, u32[]{:S(2)}, u32[]{:S(2)}) collective-permute-start(f32[12,2,3,2048]{3,1,2,0:T(2,128)S(1)} %copy.22), channel_id=1, source_target_pairs={{0,1},{1,2},{2,3},{3,4},{4,5},{5,6},{6,7},{7,8},{8,9},{9,10},{10,1... | collective-permute-start | bytes 1769480 | tf_op jit(solution)/shard_map/ppermute | solution.py:34
  259.6 17.1 %collective-permute-start.1 = (f32[12,2,3,2048]{3,1,2,0:T(2,128)S(1)}, f32[12,2,3,2048]{3,1,2,0:T(2,128)S(1)}, u32[]{:S(2)}, u32[]{:S(2)}) collective-permute-start(f32[12,2,3,2048]{3,1,2,0:T(2,128)S(1)} %copy.23), channel_id=1, source_target_pairs={{1,0},{2,1},{3,2},{4,3},{5,4},{6,5},{7,6},{8,7},{9,8},{10,9},{11,1... | collective-permute-start | bytes 1769480 | tf_op jit(solution)/shard_map/ppermute | solution.py:37
  263.6 11.7 %collective-permute-start.2 = (f32[2,2,3,2048]{3,2,1,0:T(4,128)S(1)}, f32[2,2,3,2048]{3,2,1,0:T(4,128)}, u32[]{:S(2)}, u32[]{:S(2)}) collective-permute-start(f32[2,2,3,2048]{3,2,1,0:T(4,128)S(1)} %get-tuple-element.31), channel_id=1, source_target_pairs={{0,1},{1,2},{2,3},{3,4},{4,5},{5,6},{6,7},{7,8},{8,9},{9,10},{10,1... | collective-permute-start | bytes 294920 | tf_op jit(solution)/shard_map/ppermute | solution.py:34
  277.1 2.8 copy-start

commit v2 on v0

v2 whole, which is shorter than its diff:
```python
import math

import jax
import jax.numpy as jnp
from jax import lax
from jax.experimental import pallas as pl
from jax.experimental.pallas import tpu as pltpu
from jax.sharding import PartitionSpec as P

M = 1024
NLAT = 1024
NLON = 2048
LAYER_TOTAL = 8
NF = 4
NTR = 12
TLEV = 2
PAIRS = 512


COURANT = 0.15
DRAG_COEFFICIENT = 0.2
MOISTURE_SOURCE = 0.3
RAINFALL_FACTOR = 0.2
HIGH = lax.Precision.HIGH

HALO = 3
EDGE = 8


def split_orders(pair_ids):
    low_even = pair_ids % 2 == 0
    even = jnp.where(low_even, pair_ids, M - 1 - pair_ids)
    return low_even, even, M - 1 - even


def half_tables(orders, points):
    step = 128
    coarse_ids = jnp.arange(points // step, dtype=jnp.int32) * step
    fine_ids = jnp.arange(step, dtype=jnp.int32)
    unit = 2.0 * math.pi / NLON
    coarse = (orders[:, None] * coarse_ids[None, :] % NLON).astype(jnp.float32) * unit
    fine = (orders[:, None] * fine_ids[None, :] % NLON).astype(jnp.float32) * unit
    factor = 1.0 / math.sqrt(NLON)
    cc, sc = lax.optimization_barrier((jnp.cos(coarse) * factor, jnp.sin(coarse) * factor))
    cf, sf = lax.optimization_barrier((jnp.cos(fine), jnp.sin(fine)))
    cos = [cc[:, a : a + 1] * cf - sc[:, a : a + 1] * sf for a in range(points // step)]
    sin = [-(sc[:, a : a + 1] * cf + cc[:, a : a + 1] * sf) for a in range(points // step)]
    return jnp.stack([jnp.concatenate(cos, axis=1), jnp.concatenate(sin, axis=1)], axis=0)


MESH = pl.DeviceIdType.MESH
GROUP = 8
RING = 4
LATS = 8
UNIT = 2
PART = NF * LAYER_TOTAL


def partner(index, count, step):
    if step == 1:
        return index + 1 - 2 * (index % 2)
    if step == 2:
        return (index + count // 2) % count
    return count - 1 - index


def split(x):
    high = x.astype(jnp.bfloat16)
    return high, (x - high.astype(jnp.float32)).astype(jnp.bfloat16)


def product(left, right, contract):
    dims = ((contract[:1], contract[1:]), ((), ()))
    rows = left.shape[0]
    left_high, left_low = split(left)
    right_high, right_low = split(right)
    both = lax.dot_general(
        jnp.concatenate([left_high, left_low], axis=0), right_high, dims,
        preferred_element_type=jnp.float32,
    )
    rest = lax.dot_general(left_high, right_low, dims, preferred_element_type=jnp.float32)
    return both[:rows] + (both[rows:] + rest)


def rows_of(ref, start, count):
    return jnp.concatenate(
        [ref[pl.ds(2 * start, count, 2), :], ref[pl.ds(2 * start + 1, count, 2), :]], axis=1
    )


def order_rows(pair_ref, slot, first, count):
    pair = pair_ref[slot]
    bound = M - pair
    low_even = pair % 2 == 0
    even_from, even_to = jnp.where(low_even, 0, bound), jnp.where(low_even, bound, M + 1)
    odd_from, odd_to = jnp.where(low_even, bound, 0), jnp.where(low_even, M + 1, bound)
    rows = first + lax.broadcasted_iota(jnp.int32, (1, count), 1)
    even = (rows >= even_from) & (rows < even_to)
    odd = (rows >= odd_from) & (rows < odd_to)
    return even, odd, jnp.where(pair == 0, 1.0, 2.0)


def fourier_tables(pair_of_slot):
    _, even_all, odd_all = split_orders(pair_of_slot)
    half = NLON // 2
    tables = jnp.stack([half_tables(even_all, half), half_tables(odd_all, half)], axis=0)
    tables = tables.reshape(2, -1, half)
    high = lax.reduce_precision(tables, 8, 7)
    return high.astype(jnp.bfloat16), (tables - high).astype(jnp.bfloat16)


def transport_kernel(
    first_ref, rate_ref, q_ref, ql_ref, qh_ref, u_ref, ul_ref, uh_ref, w_ref, wl_ref, wh_ref,
    out_ref, heat_ref, pad, ap, an, bp, bn,
):
    rows = q_ref.shape[2]
    total = rows + EDGE
    lons = q_ref.shape[3]
    level = pl.program_id(0)
    tracer = pl.program_id(1)
    edge_rows = lax.broadcasted_iota(jnp.int32, (EDGE, lons), 0)

    @pl.when(tracer == 0)
    def _():
        pad[0:EDGE, :] = jnp.where(edge_rows < EDGE // 2, uh_ref[0], ul_ref[0])
        pad[EDGE:total, :] = u_ref[0]
        u = pad[...]
        face = (0.5 * COURANT) * (u + pltpu.roll(u, lons - 1, 1))
        ap[...] = jnp.maximum(face, 0.0)
        an[...] = jnp.minimum(face, 0.0)
        pad[0:EDGE, :] = jnp.where(edge_rows < EDGE // 2, wh_ref[0], wl_ref[0])
        pad[EDGE:total, :] = w_ref[0]
        w = pad[...]
        face = (-0.5 * COURANT) * (w + pltpu.roll(w, total - 1, 0))
        place = lax.broadcasted_iota(jnp.int32, (total, lons), 0)
        upper = first_ref[0] + jnp.where(place < EDGE // 2, rows + place, place - EDGE)
        inside = (upper >= 0) & (upper <= NLAT - 2)
        bp[...] = jnp.where(inside, jnp.maximum(face, 0.0), 0.0)
        bn[...] = jnp.where(inside, jnp.minimum(face, 0.0), 0.0)
        pad[0:EDGE, :] = jnp.zeros((EDGE, lons), jnp.float32)

    def step(q):
        east = ap[...] * q + an[...] * pltpu.roll(q, lons - 1, 1)
        south = bp[...] * q + bn[...] * pltpu.roll(q, total - 1, 0)
        return q - ((east - pltpu.roll(east, 1, 1)) + (south - pltpu.roll(south, 1, 0)))

    pad[0:HALO, :] = qh_ref[0, 0]
    pad[EDGE - HALO : EDGE, :] = ql_ref[0, 0]
    pad[EDGE:total, :] = q_ref[0, 0]
    q = pad[...]
    second = 0.75 * q + 0.25 * step(step(q))
    third = step(second)[EDGE:total]
    new = q_ref[0, 0] * (1.0 / 3.0) + (2.0 / 3.0) * third
    out_ref[0, 0] = new
    warm = rate_ref[tracer, level] * new

    @pl.when(tracer == 0)
    def _():
        heat_ref[0] = warm

    @pl.when(tracer > 0)
    def _():
        heat_ref[0] += warm


def transport(first_row, heat_rate, tracers, low, high, wind, wind_low, wind_high):
    count, levels, rows, lons = tracers.shape
    total = rows + EDGE

    def tracer_spec(height):
        return pl.BlockSpec((1, 1, height, lons), lambda l, k: (k, l, 0, 0))

    def wind_spec(height, first):
        return pl.BlockSpec((1, height, lons), lambda l, k: (l + first, 0, 0))

    smem = pl.BlockSpec(memory_space=pltpu.SMEM)
    return pl.pallas_call(
        transport_kernel,
        grid=(levels, count),
        in_specs=[smem, smem]
        + [tracer_spec(rows), tracer_spec(HALO), tracer_spec(HALO)]
        + [wind_spec(rows, 0), wind_spec(EDGE, 0), wind_spec(EDGE, 0)]
        + [wind_spec(rows, levels), wind_spec(EDGE, levels), wind_spec(EDGE, levels)],
        out_specs=[tracer_spec(rows), wind_spec(rows, 0)],
        out_shape=[
            jax.ShapeDtypeStruct(tracers.shape, tracers.dtype),
            jax.ShapeDtypeStruct((levels, rows, lons), tracers.dtype),
        ],
        scratch_shapes=[pltpu.VMEM((total, lons), jnp.float32)] * 5,
        compiler_params=pltpu.CompilerParams(
            dimension_semantics=("arbitrary", "arbitrary"), vmem_limit_bytes=40 * 1024 * 1024
        ),
    )(
        first_row.reshape(1), heat_rate, tracers, low, high,
        wind, wind_low, wind_high, wind, wind_low, wind_high,
    )


def neighbour(band, count, quarter, quarters, step):
    place = (band * quarters + quarter + step + count * quarters) % (count * quarters)
    return {"ma": place // quarters, "pb": place % quarters}


def enter(band_count, here, quarter_count, quarter, beside):
    barrier = pltpu.get_barrier_semaphore()
    others = [{"ma": (here + step) % band_count} for step in range(1, band_count)]
    others += [{"pb": partner(quarter, quarter_count, step)} for step in (1, 2)]
    for other in others + beside:
        pl.semaphore_signal(barrier, inc=1, device_id=other, device_id_type=MESH)
    pl.semaphore_wait(barrier, len(others) + len(beside))


def stream_rows(legendre_ref, held, sem, slot):
    return pltpu.make_async_copy(legendre_ref.at[slot], held.at[slot % RING], sem.at[slot % RING])


def wait_bytes(ref, sem):
    pltpu.make_async_copy(ref, ref, sem).wait()


def to_grid(spectral_ref, high_ref, low_ref, out_ref, left):
    sources, chunks = spectral_ref.shape[:2]
    slots = sources * chunks * GROUP
    half = high_ref.shape[2]
    for j in range(LATS):
        block = spectral_ref[:, :, j * GROUP : (j + 1) * GROUP, :].reshape(slots, 4 * PART).T
        for h in range(2):
            for p in range(2):
                left[h, j * PART : (j + 1) * PART, p * slots : (p + 1) * slots] = block[
                    (2 * h + p) * PART : (2 * h + p + 1) * PART
                ]
    sums = []
    for h in range(2):
        high, low = split(left[h])
        dot = lambda a, b: jnp.dot(a, b, preferred_element_type=jnp.float32)
        sums.append(dot(high, high_ref[h]) + (dot(low, high_ref[h]) + dot(high, low_ref[h])))
    out_ref[:, :half] = sums[0] + sums[1]
    out_ref[:, half:] = sums[0] - sums[1]


def from_grid(field_ref, heat_ref, first, high_ref, low_ref, out_ref, left, turned):
    sources, chunks = out_ref.shape[:2]
    slots = sources * chunks * GROUP
    half = high_ref.shape[2]
    lev = LAYER_TOTAL
    level = lax.broadcasted_iota(jnp.int32, (lev, half), 0)

    for j in range(LATS):
        def tendency(start):
            cols = slice(start, start + half)
            at = lambda f: field_ref[j * PART + f * lev : j * PART + (f + 1) * lev, cols]
            u, v, t, q = at(0), at(1), at(2), at(3)
            speed = jnp.sqrt(u * u + v * v + 1.0)
            moist = MOISTURE_SOURCE * t * q
            warm = jnp.zeros((lev, half), jnp.float32)
            for l in range(TLEV):
                rows = heat_ref[l, pl.ds(first, LATS), cols]
                warm = jnp.where(level == l, rows[j : j + 1], warm)
            return jnp.concatenate(
                [
                    -DRAG_COEFFICIENT * speed * u,
                    -DRAG_COEFFICIENT * speed * v,
                    warm - moist,
                    moist - RAINFALL_FACTOR * speed * q,
                ],
                axis=0,
            )

        near = tendency(0)
        far = tendency(half)
        left[0, j * PART : (j + 1) * PART] = near + far
        left[1, j * PART : (j + 1) * PART] = near - far
    dims = (((1,), (1,)), ((), ()))
    for h in range(2):
        high, low = split(left[h])
        dot = lambda a, b: lax.dot_general(a, b, dims, preferred_element_type=jnp.float32)
        both = dot(high, high_ref[h]) + (dot(low, high_ref[h]) + dot(high, low_ref[h]))
        for j in range(LATS):
            for p in range(2):
                turned[j, (2 * h + p) * PART : (2 * h + p + 1) * PART] = both[
                    j * PART : (j + 1) * PART, p * slots : (p + 1) * slots
                ]
    for j in range(LATS):
        out_ref[:, :, j * GROUP : (j + 1) * GROUP, :] = turned[j].T.reshape(
            sources, chunks, GROUP, 4 * PART
        )


def analysis_kernel(
    pair_ref, coefs_ref, legendre_ref, high_ref, low_ref, above_ref, below_ref,
    field_ref, wind_ref, wind_low_ref, wind_high_ref, trace_low_ref, trace_high_ref, bands_ref,
    pieces, held, sums, high, low, block, left, field, wind,
    load_sem, own_sem, near_send, near_recv, far_send, far_recv,
    pass_send, pass_recv, send_sem, recv_sem, keep_sem, table_sem, trace_send, trace_recv,
    block_sem, field_sem, wind_sem, edge_send, edge_recv,
):
    slots, columns, piece = coefs_ref.shape
    chunks = slots // GROUP
    count = lax.axis_size("ma")
    here = lax.axis_index("ma")
    quarters = lax.axis_size("pb")
    quarter = lax.axis_index("pb")
    near, far = partner(quarter, quarters, 1), partner(quarter, quarters, 2)
    after = neighbour(here, count, quarter, quarters, 1)
    before = neighbour(here, count, quarter, quarters, -1)
    band = sums.shape[1] // count
    width = sums.shape[1] // GROUP
    weight_columns = 2 * columns
    groups = band // (LATS * GROUP)
    late = LATS * GROUP
    early = band - late
    spans = ((0, early), (early, late))

    def part(ref, chunk):
        return ref.at[pl.ds(chunk * GROUP, GROUP)]

    def remote(source, target, sends, receives, device):
        return pltpu.make_async_remote_copy(
            source, target, sends, receives, device_id=device, device_id_type=MESH
        )

    def own(chunk):
        return pltpu.make_async_copy(
            part(coefs_ref, chunk), part(pieces.at[0], chunk), own_sem.at[chunk]
        )

    def to_near(chunk):
        return remote(
            part(coefs_ref, chunk), part(pieces.at[1], chunk),
            near_send.at[chunk], near_recv.at[chunk], {"pb": near},
        )

    def to_far(chunk):
        return remote(
            part(coefs_ref, chunk), part(pieces.at[2], chunk),
            far_send.at[chunk], far_recv.at[chunk], {"pb": far},
        )

    def pass_on(chunk):
        return remote(
            part(pieces.at[2], chunk), part(pieces.at[3], chunk),
            pass_send.at[chunk], pass_recv.at[chunk], {"pb": near},
        )

    def send_bands(chunk, which):
        start, size = spans[which]
        for step in range(1, count):
            target = (here + step) % count
            remote(
                sums.at[chunk, pl.ds(target * band + start, size)],
                bands_ref.at[here, chunk, pl.ds(start, size)],
                send_sem.at[which], recv_sem.at[which], {"ma": target},
            ).start()
        pltpu.make_async_copy(
            sums.at[chunk, pl.ds(here * band + start, size)],
            bands_ref.at[here, chunk, pl.ds(start, size)],
            keep_sem.at[which],
        ).start()

    def wait_bands(which):
        start, size = spans[which]
        wait_bytes(bands_ref.at[pl.ds(0, count - 1), :, pl.ds(start, size)], recv_sem.at[which])
        wait_bytes(bands_ref.at[0, :, pl.ds(start, size)], keep_sem.at[which])

    tables = [
        pltpu.make_async_copy(high_ref, high, table_sem.at[0]),
        pltpu.make_async_copy(low_ref, low, table_sem.at[1]),
    ]
    traces = [
        remote(above_ref, trace_high_ref, trace_send.at[0], trace_recv.at[0], before),
        remote(below_ref, trace_low_ref, trace_send.at[1], trace_recv.at[1], after),
    ]

    for slot in range(RING - 1):
        stream_rows(legendre_ref, held, load_sem, slot).start()
    enter(count, here, quarters, quarter, [after, before])

    def begin(chunk, carry):
        to_far(chunk).start()
        to_near(chunk).start()
        own(chunk).start()
        return carry

    lax.fori_loop(0, chunks, begin, 0)

    def one_slot(slot, chunk):
        stream_rows(legendre_ref, held, load_sem, slot).wait()

        @pl.when(slot + RING - 1 < slots)
        def _():
            stream_rows(legendre_ref, held, load_sem, slot + RING - 1).start()

        rows = held.at[slot % RING]
        total = jnp.zeros((weight_columns, width), jnp.float32)
        for k in range(quarters):
            first = (quarter if k == 0 else partner(quarter, quarters, k)) * piece
            even, odd, even_weight = order_rows(pair_ref, slot, first, piece)
            x = pieces[k, slot]
            both = jnp.concatenate(
                [jnp.where(even, x * even_weight, 0.0), jnp.where(odd, x * 2.0, 0.0)], axis=0
            )
            total = total + product(both, rows_of(rows, first, piece), (1, 0))
        sums[chunk, pl.ds(slot % GROUP, width, GROUP), :] = total.T

    def one_chunk(chunk, carry):
        to_far(chunk).wait_recv()
        pass_on(chunk).start()
        own(chunk).wait()
        to_near(chunk).wait_recv()
        pass_on(chunk).wait_recv()

        def body(i, inner):
            one_slot(chunk * GROUP + i, chunk)
            return inner

        lax.fori_loop(0, GROUP, body, 0)
        if early:
            send_bands(chunk, 0)
        return carry

    lax.fori_loop(0, chunks, one_chunk, 0)

    def send_late(chunk, carry):
        send_bands(chunk, 1)
        return carry

    lax.fori_loop(0, chunks, send_late, 0)
    for copy in tables + traces:
        copy.start()

    def load(group):
        return pltpu.make_async_copy(
            bands_ref.at[:, :, pl.ds(group * late, late)], block.at[group % 2],
            block_sem.at[group % 2],
        )

    def store(group):
        return pltpu.make_async_copy(
            field.at[group % 2], field_ref.at[pl.ds(group * LATS * PART, LATS * PART)],
            field_sem.at[group % 2],
        )

    for copy in tables:
        copy.wait()
    wait_bands(0 if early else 1)
    load(0).start()

    def one_group(group, carry):
        load(group).wait()

        @pl.when(group + 2 < groups)
        def _():
            load(group + 1).start()

        @pl.when(group + 2 == groups)
        def _():
            wait_bands(1)
            load(group + 1).start()

        @pl.when(group >= 2)
        def _():
            store(group - 2).wait()

        to_grid(block.at[group % 2], high, low, field.at[group % 2], left)
        store(group).start()
        for component in range(2):
            for l in range(TLEV):
                row = component * LAYER_TOTAL + l
                wind[component * TLEV + l, pl.ds(group * LATS, LATS), :] = jnp.concatenate(
                    [
                        field[group % 2, j * PART + row : j * PART + row + 1, :]
                        for j in range(LATS)
                    ],
                    axis=0,
                )
        return carry

    lax.fori_loop(0, groups, one_group, 0)
    lats = groups * LATS
    edges = [
        remote(
            wind.at[:, pl.ds(0, EDGE)], wind_high_ref, edge_send.at[0], edge_recv.at[0], before
        ),
        remote(
            wind.at[:, pl.ds(lats - EDGE, EDGE)], wind_low_ref,
            edge_send.at[1], edge_recv.at[1], after,
        ),
    ]
    winds = pltpu.make_async_copy(wind, wind_ref, wind_sem)
    for copy in edges + [winds]:
        copy.start()

    def finish(chunk, carry):
        to_far(chunk).wait_send()
        to_near(chunk).wait_send()
        pass_on(chunk).wait_send()
        return carry

    lax.fori_loop(0, chunks, finish, 0)
    for which in range(0 if early else 1, 2):
        start, size = spans[which]
        wait_bytes(bands_ref.at[pl.ds(0, count - 1), :, pl.ds(start, size)], send_sem.at[which])
    for group in range(max(groups - 2, 0), groups):
        store(group).wait()
    for copy in traces + edges + [winds]:
        copy.wait()


def analysis(pairs, coefs, legendre, high, low, above, below, band_count):
    slots, columns, piece = coefs.shape
    chunks = slots // GROUP
    half_rows, lanes = legendre.shape[1:]
    quarters = half_rows // (2 * piece)
    width = 2 * lanes
    lats = width // band_count
    any_space = pl.BlockSpec(memory_space=pl.ANY)
    dma = pltpu.SemaphoreType.DMA
    shape = lambda *dims: jax.ShapeDtypeStruct(dims, jnp.float32)
    late = LATS * GROUP
    return pl.pallas_call(
        analysis_kernel,
        in_specs=[pl.BlockSpec(memory_space=pltpu.SMEM)] + [any_space] * 6,
        out_specs=[any_space] * 7,
        out_shape=[
            shape(lats * PART, NLON),
            shape(2 * TLEV, lats, NLON),
            shape(2 * TLEV, EDGE, NLON),
            shape(2 * TLEV, EDGE, NLON),
            shape(*below.shape),
            shape(*above.shape),
            shape(band_count, chunks, lats * GROUP, 2 * columns),
        ],
        scratch_shapes=[
            pltpu.VMEM((quarters, slots, columns, piece), jnp.float32),
            pltpu.VMEM((RING, half_rows, lanes), jnp.float32),
            pltpu.VMEM((chunks, width * GROUP, 2 * columns), jnp.float32),
            pltpu.VMEM(high.shape, high.dtype),
            pltpu.VMEM(low.shape, low.dtype),
            pltpu.VMEM((2, band_count, chunks, late, 2 * columns), jnp.float32),
            pltpu.VMEM((2, LATS * PART, high.shape[1]), jnp.float32),
            pltpu.VMEM((2, LATS * PART, NLON), jnp.float32),
            pltpu.VMEM((2 * TLEV, lats, NLON), jnp.float32),
            dma((RING,)),
        ]
        + [dma((chunks,))] * 7
        + [dma((2,))] * 8
        + [dma(())]
        + [dma((2,))] * 2,
        compiler_params=pltpu.CompilerParams(
            collective_id=0, has_side_effects=True, vmem_limit_bytes=63 * 1024 * 1024
        ),
    )(pairs, coefs, legendre, high, low, above, below)


def synthesis_kernel(
    pair_ref, quad_ref, heat_ref, field_ref, high_ref, low_ref, legendre_ref,
    out_ref, fourier_ref,
    bands, held, near_held, far_held, load_sem, send_sem, recv_sem, keep_sem,
    near_send, near_recv, far_send, far_recv, out_sem, table_sem, field_sem, turn_sem,
):
    slots, columns, piece = out_ref.shape
    chunks = slots // GROUP
    units = slots // UNIT
    count = lax.axis_size("ma")
    here = lax.axis_index("ma")
    quarters = lax.axis_size("pb")
    quarter = lax.axis_index("pb")
    near, far = partner(quarter, quarters, 1), partner(quarter, quarters, 2)
    band = bands.shape[1] // count
    width = bands.shape[1] // GROUP
    first_rows = LATS * GROUP
    groups = band // first_rows

    def remote(source, target, sends, receives, device):
        return pltpu.make_async_remote_copy(
            source, target, sends, receives, device_id=device, device_id_type=MESH
        )

    def send_orders(chunk, start, size):
        for step in range(1, count):
            target = (here + step) % count
            remote(
                fourier_ref.at[target, chunk, pl.ds(start, size)],
                bands.at[chunk, pl.ds(here * band + start, size)],
                send_sem, recv_sem.at[chunk], {"ma": target},
            ).start()
        pltpu.make_async_copy(
            fourier_ref.at[here, chunk, pl.ds(start, size)],
            bands.at[chunk, pl.ds(here * band + start, size)],
            keep_sem.at[chunk],
        ).start()

    for slot in range(RING - 1):
        stream_rows(legendre_ref, held, load_sem, slot).start()

    def turn(high, low, field, left, turned, block):
        tables = [
            pltpu.make_async_copy(high_ref, high, table_sem.at[0]),
            pltpu.make_async_copy(low_ref, low, table_sem.at[1]),
        ]

        def load(group):
            return pltpu.make_async_copy(
                field_ref.at[pl.ds(group * LATS * PART, LATS * PART)], field.at[group % 2],
                field_sem.at[group % 2],
            )

        def store(group):
            return pltpu.make_async_copy(
                block.at[group % 2],
                fourier_ref.at[:, :, pl.ds(group * first_rows, first_rows)],
                turn_sem.at[group % 2],
            )

        load(0).start()
        for copy in tables:
            copy.start()
        enter(count, here, quarters, quarter, [])
        for copy in tables:
            copy.wait()

        def one_group(group, carry):
            load(group).wait()

            @pl.when(group + 1 < groups)
            def _():
                load(group + 1).start()

            @pl.when(group >= 3)
            def _():
                store(group - 2).wait()

            from_grid(
                field.at[group % 2], heat_ref, pl.multiple_of(group * LATS, LATS), high, low,
                block.at[group % 2], left, turned,
            )
            store(group).start()

            @pl.when(group == 0)
            def _():
                store(group).wait()

                def first(chunk, inner):
                    send_orders(chunk, 0, first_rows)
                    return inner

                lax.fori_loop(0, chunks, first, 0)

            return carry

        lax.fori_loop(0, groups, one_group, 0)
        for group in range(max(groups - 2, 1), groups):
            store(group).wait()

    pl.run_scoped(
        turn,
        pltpu.VMEM(high_ref.shape, high_ref.dtype),
        pltpu.VMEM(low_ref.shape, low_ref.dtype),
        pltpu.VMEM((2, LATS * PART, NLON), jnp.float32),
        pltpu.VMEM((2, LATS * PART, NLON // 2), jnp.float32),
        pltpu.VMEM((LATS, 4 * PART, count * slots), jnp.float32),
        pltpu.VMEM((2, count, chunks, first_rows, 4 * PART), jnp.float32),
    )

    def rest(chunk, carry):
        send_orders(chunk, first_rows, band - first_rows)
        return carry

    if groups > 1:
        lax.fori_loop(0, chunks, rest, 0)

    def sum_up(parts):
        def to_near(unit, k):
            return remote(
                parts.at[unit, 2 * k + 1], near_held.at[unit, k],
                near_send.at[k, unit], near_recv.at[k, unit], {"pb": near},
            )

        def to_far(unit):
            return remote(
                parts.at[unit, 2], far_held.at[unit], far_send.at[unit], far_recv.at[unit],
                {"pb": far},
            )

        def store(unit):
            return pltpu.make_async_copy(
                parts.at[unit, 0], out_ref.at[pl.ds(unit * UNIT, UNIT)], out_sem.at[unit]
            )

        def one_slot(slot, unit, own):
            stream_rows(legendre_ref, held, load_sem, slot).wait()

            @pl.when(slot + RING - 1 < slots)
            def _():
                stream_rows(legendre_ref, held, load_sem, slot + RING - 1).start()

            rows = held.at[slot % RING]
            weighted = bands[slot // GROUP, pl.ds(slot % GROUP, width, GROUP), :].T * quad_ref[...]
            for k in range(quarters):
                first = (quarter if k == 0 else partner(quarter, quarters, k)) * piece
                even, odd, _ = order_rows(pair_ref, slot, first, piece)
                both = product(weighted, rows_of(rows, first, piece), (1, 1))
                parts[unit, k, own] = jnp.where(
                    even, both[:columns], jnp.where(odd, both[columns:], 0.0)
                )

        def advance(unit):
            to_near(unit, 1).wait_recv()
            for i in range(UNIT):
                parts[unit, 2, i] = parts[unit, 2, i] + near_held[unit, 1, i]
            to_far(unit).start()

        def complete(unit):
            to_near(unit, 0).wait_recv()
            to_far(unit).wait_recv()
            for i in range(UNIT):
                parts[unit, 0, i] = (
                    parts[unit, 0, i] + near_held[unit, 0, i] + far_held[unit, i]
                )
            store(unit).start()

        lag = 2 * (GROUP // UNIT)

        def one_unit(unit, carry):
            @pl.when(unit % (GROUP // UNIT) == 0)
            def _():
                chunk = unit // (GROUP // UNIT)
                wait_bytes(bands.at[chunk, pl.ds(0, band)], keep_sem.at[chunk])
                wait_bytes(bands.at[chunk, pl.ds(0, (count - 1) * band)], recv_sem.at[chunk])

            def body(i, inner):
                one_slot(unit * UNIT + i, unit, i)
                return inner

            lax.fori_loop(0, UNIT, body, 0)
            to_near(unit, 1).start()
            to_near(unit, 0).start()

            @pl.when(unit > 0)
            def _():
                advance(unit - 1)

            @pl.when(unit >= lag)
            def _():
                complete(unit - lag)

            return carry

        lax.fori_loop(0, units, one_unit, 0)
        advance(units - 1)

        def last(i, carry):
            complete(units - lag + i)
            return carry

        lax.fori_loop(0, lag, last, 0)

        def finish(unit, carry):
            to_near(unit, 0).wait_send()
            to_near(unit, 1).wait_send()
            to_far(unit).wait_send()
            store(unit).wait()
            return carry

        lax.fori_loop(0, units, finish, 0)
        wait_bytes(fourier_ref.at[pl.ds(0, count - 1)], send_sem)

    pl.run_scoped(sum_up, pltpu.VMEM((units, quarters, UNIT, columns, piece), jnp.float32))


def synthesis(pairs, quad, heat, field, high, low, legendre, piece, band_count):
    slots = pairs.shape[0]
    chunks = slots // GROUP
    units = slots // UNIT
    lats = heat.shape[1]
    columns = 2 * PART
    half_rows, lanes = legendre.shape[1:]
    any_space = pl.BlockSpec(memory_space=pl.ANY)
    vmem = pl.BlockSpec(memory_space=pltpu.VMEM)
    dma = pltpu.SemaphoreType.DMA
    block = (UNIT, columns, piece)
    return pl.pallas_call(
        synthesis_kernel,
        in_specs=[pl.BlockSpec(memory_space=pltpu.SMEM), vmem, vmem] + [any_space] * 4,
        out_specs=[any_space] * 2,
        out_shape=[
            jax.ShapeDtypeStruct((slots, columns, piece), jnp.float32),
            jax.ShapeDtypeStruct((band_count, chunks, lats * GROUP, 2 * columns), jnp.float32),
        ],
        scratch_shapes=[
            pltpu.VMEM((chunks, band_count * lats * GROUP, 2 * columns), jnp.float32),
            pltpu.VMEM((RING, half_rows, lanes), jnp.float32),
            pltpu.VMEM((units, 2) + block, jnp.float32),
            pltpu.VMEM((units,) + block, jnp.float32),
            dma((RING,)),
            dma(()),
            dma((chunks,)),
            dma((chunks,)),
            dma((2, units)),
            dma((2, units)),
            dma((units,)),
            dma((units,)),
            dma((units,)),
            dma((2,)),
            dma((2,)),
            dma((2,)),
        ],
        compiler_params=pltpu.CompilerParams(
            collective_id=1, has_side_effects=True, vmem_limit_bytes=63 * 1024 * 1024
        ),
    )(pairs, quad, heat, field, high, low, legendre)[0]


def shards(coefs, legendre, quad_weight, pair_of_slot, tracers, heat_rate):
    slot_count, piece = coefs.shape[:2]
    quarter = legendre.shape[3]
    band_count = lax.axis_size("ma")
    band_rows = tracers.shape[2]
    lanes = 128
    legendre_rows = legendre.reshape(slot_count, -1, lanes)
    own_pairs = lax.dynamic_slice_in_dim(
        pair_of_slot, lax.axis_index("ma") * slot_count, slot_count, 0
    )
    table_high, table_low = fourier_tables(pair_of_slot)
    field, wind, wind_low, wind_high, low, high, _ = analysis(
        own_pairs, jnp.transpose(coefs, (0, 2, 1)), legendre_rows, table_high, table_low,
        tracers[:, :, :HALO], tracers[:, :, band_rows - HALO :], band_count,
    )
    first_row = (lax.axis_index(("ma", "pb")) * band_rows).astype(jnp.int32)
    new_tracers, heating = transport(
        first_row, heat_rate, tracers, low, high, wind, wind_low, wind_high
    )
    spec = synthesis(
        own_pairs, quad_weight.reshape(1, quarter), heating, field, table_high, table_low,
        legendre_rows, piece, band_count,
    )
    return (jnp.transpose(spec, (0, 2, 1)), new_tracers)


def solution(mesh):
    in_specs = (
        P("ma", "pb", None),
        P("ma", None, "pb", None),
        P("pb", None),
        P(),
        P(None, None, ("ma", "pb"), None),
        P(),
    )
    out_specs = (P("ma", "pb", None), P(None, None, ("ma", "pb"), None))
    return jax.shard_map(shards, mesh=mesh, in_specs=in_specs, out_specs=out_specs, check_vma=False)
```

time: 1220 us -> 559 us (0.46)
  waiting for transfers between devices: 775 us -> 0 us
  Pallas kernels: 24.9 us -> 525 us
  matrix products: 162 us -> 0 us
  other arithmetic: 97 us -> 11.5 us
  local copies, waits for them, and re-layouts: 89.9 us -> 20.7 us
  starting transfers between devices: 46 us -> 0 us
  between operations: 15 us -> 0.83 us
    pallas_call x0 -> x2, Pallas kernels: none -> 502 us  [the longest x1 262 us: synthesis(): pl.pallas_call(synthesis_kernel, in_specs=[pl.BlockSpec(memory_space=pltp...]
    all_to_all x2 -> x0, waiting for transfers between devices: 324 us -> none  [the longest x1 179 us: shards(): lax.all_to_all(fourier, 'ma', split_axis=0, concat_axis=1, tiled=True)]
    reduce_scatter x1 -> x0, waiting for transfers between devices: 240 us -> none  [shards(): lax.psum_scatter(jnp.where(even_rows.T[:, :, None], row_sums[:, :, :colum...]
    all_gather x1 -> x0, waiting for transfers between devices: 209 us -> none  [shards(): row_piece = lax.all_gather(coefs, 'pb', axis=1, tiled=True)]
    dot_general x6 -> x0, matrix products: 162 us -> none  [the longest x1 71.7 us: shards(): jnp.einsum('srl,src->slc', legendre_rows, masked, precision=HIGH)]
    add x2 -> x0, other arithmetic: 38 us -> none  [the longest x1 36.9 us: shards(): jnp.where(even_rows.T[:, :, None], row_sums[:, :, :columns], 0.0)]
    select_n x2 -> x0, other arithmetic: 35 us -> none  [the longest x1 34.9 us: shards(): jnp.where(even_rows[:, :, None], row_piece * even_weight, 0.0)]
    ppermute x4 -> x0, starting transfers between devices: 25.8 us -> none  [the longest x2 21.9 us: halo_rows(): lax.ppermute(lax.slice_in_dim(block, 0, width, axis=dim), axes, backward)]
  transfers between devices with their start and end apart: 8 -> 0, of which waited for: 5 -> 0; matrix products, arithmetic and copies ran while one was open for 6% -> 0% of each run, Pallas kernels for 0% -> 0%
where the time goes in v2:
time: 559 us; the launch traced here: 558 us
  Pallas kernels  525 us (94%)
  local copies, waits for them, and re-layouts  20.7 us (4%)
  other arithmetic  11.5 us (2%)
    pallas_call x1, Pallas kernels, synthesis(): pl.pallas_call(synthesis_kernel, in_specs=[pl.BlockSpec(memory_space=pltp...  262 us
    pallas_call x1, Pallas kernels, analysis(): pl.pallas_call(analysis_kernel, in_specs=[pl.BlockSpec(memory_space=pltpu...  241 us
    pallas_call x1, Pallas kernels, transport(): pl.pallas_call(transport_kernel, grid=(levels, count), in_specs=[smem, sm...  22.9 us
    unnamed x16, local copies, waits for them, and re-layouts  16 us

profile of v2, /device:TPU:12, one launch (start us, length us, event | category | flops | bytes accessed | tf_op | source)
XLA Modules:
  0.0 558.1 jit_solution(17759118123527621798)
XLA Ops:
  0.6 1.3 dynamic_slice.3.pair_ref
  1.9 0.7 broadcast_subtract_fusion
  2.6 0.8 copy.9.rate_ref
  3.4 0.2 sine_multiply_fusion.1
  3.7 2.1 fusion.13
  5.8 3.4 fusion.25
  9.4 0.2 subtract_dynamic-update-slice_fusion.14
  9.8 0.2 subtract_dynamic-update-slice_fusion.12
  10.0 0.2 subtract_dynamic-update-slice_fusion.11
  10.2 0.2 subtract_dynamic-update-slice_fusion.10
  10.4 0.2 subtract_dynamic-update-slice_fusion.9
  10.6 0.2 subtract_dynamic-update-slice_fusion.8
  10.8 0.3 pad_maximum_fusion.1
  11.2 0.2 subtract_dynamic-update-slice_fusion.7
  11.4 0.2 subtract_dynamic-update-slice_fusion.6
  11.6 0.2 subtract_dynamic-update-slice_fusion.5
  11.8 0.2 subtract_dynamic-update-slice_fusion.4
  12.0 0.2 subtract_dynamic-update-slice_fusion.3
  12.4 0.2 subtract_dynamic-update-slice_fusion.1
  12.9 0.3 pad_maximum_fusion.2
  13.2 4.6 fusion
  17.7 240.6 %shard_map.77 = (f32[1024,2048]{1,0:T(8,128)}, f32[4,32,2048]{2,1,0:T(8,128)}, f32[4,8,2048]{2,1,0:T(8,128)}, f32[4,8,2048]{2,1,0:T(8,128)}, f32[12,2,3,2048]{3,...) custom-call(s32[64]{0:T(128)} %dynamic_slice.3.pair_ref, f32[64,64,264]{2,1,0:T(8,128)} %bitcast.44, ...), custom_call_target="tpu_custom_call" | custom-call | tf_op jit(solution)/shard_map/pallas_call | solution.py:520
  258.3 2.8 copy-done
  261.1 1.2 copy-done.1
  262.3 0.9 copy-done.2
  263.3 0.9 copy-done.3
  264.2 1.1 copy-done.4
  265.4 1.1 copy-done.5
  266.5 22.9 %shard_map.78 = (f32[12,2,32,2048]{3,2,1,0:T(8,128)}, f32[2,32,2048]{2,1,0:T(8,128)S(1)}) custom-call(s32[1]{0:T(128)} %bitcast.first_ref, f32[12,2]{1,0:T(8,128)S(1)} %copy.9.rate_ref, f32[12,2,32,2048]{3,2,1,0:T(8,128)S(1)} %copy-done, f32[12,2,3,2048]{3,2,1,0:T(4,128)S(1)} %copy-done.4, f32[12,2,3,2048]{3,2,1,0:T(4,128)S(1)} %copy-done.5, ...), custom_call_target="tpu_custom_call" | custom-call | tf_op jit(solution)/shard_map/pallas_call | solution.py:177
  289.4 0.8 copy-done.6
  290.2 261.6 %shard_map.79 = (f32[64,64,264]{2,1,0:T(8,128)}, f32[8,8,256,128]{3,2,1,0:T(8,128)}) custom-call(s32[64]{0:T(128)} %dynamic_slice.3.pair_ref, f32[1,256]{1,0:T(1,128)} %quad_ref.1, f32[2,32,2048]{2,1,0:T(8,128)} %copy-done.6, f32[1024,2048]{1,0:T(8,128)} %get-tuple-element.33.field_ref, bf16[2,1024,1024]{2,1,0:T(8,128)(2,1)} %get-tuple-element.39.high_ref, ...), custom_call_target="tpu_custom_call" | custom-call | tf_op jit(solution)/shard_map/pallas_call | solution.py:782
  551.8 6.2 %copy.39 = f32[64,264,64]{1,2,0:T(8,128)} copy(f32[64,264,64]{1,2,0:T(8,128)} %bitcast.45) | data formatting | bytes 8650752
  (14 shorter events, 0.9 us)
Async XLA Ops:
  258.3 2.8 copy-start
  261.1 1.2 copy-start.1
  262.3 0.9 copy-start.2
  263.3 0.9 copy-start.3
  264.2 1.1 copy-start.4
  265.4 1.1 copy-start.5
  289.4 0.8 copy-start.6

commit v3 on v2

--- a/solution.py
+++ b/solution.py
@@ -188,7 +188,7 @@
         ],
         scratch_shapes=[pltpu.VMEM((total, lons), jnp.float32)] * 5,
         compiler_params=pltpu.CompilerParams(
-            dimension_semantics=("arbitrary", "arbitrary"), vmem_limit_bytes=40 * 1024 * 1024
+            dimension_semantics=("arbitrary", "arbitrary"), vmem_limit_bytes=63 * 1024 * 1024
         ),
     )(
         first_row.reshape(1), heat_rate, tracers, low, high,
@@ -392,6 +392,8 @@
 
         rows = held.at[slot % RING]
         total = jnp.zeros((weight_columns, width), jnp.float32)
+        main = piece - piece % 128
+        ends, end_rows = [], []
         for k in range(quarters):
             first = (quarter if k == 0 else partner(quarter, quarters, k)) * piece
             even, odd, even_weight = order_rows(pair_ref, slot, first, piece)
@@ -399,7 +401,12 @@
             both = jnp.concatenate(
                 [jnp.where(even, x * even_weight, 0.0), jnp.where(odd, x * 2.0, 0.0)], axis=0
             )
-            total = total + product(both, rows_of(rows, first, piece), (1, 0))
+            total = total + product(both[:, :main], rows_of(rows, first, main), (1, 0))
+            ends.append(both[:, main:])
+            end_rows.append(rows_of(rows, first + main, piece - main))
+        total = total + product(
+            jnp.concatenate(ends, axis=1), jnp.concatenate(end_rows, axis=0), (1, 0)
+        )
         sums[chunk, pl.ds(slot % GROUP, width, GROUP), :] = total.T
 
     def one_chunk(chunk, carry):
@@ -696,13 +703,26 @@
 
             rows = held.at[slot % RING]
             weighted = bands[slot // GROUP, pl.ds(slot % GROUP, width, GROUP), :].T * quad_ref[...]
-            for k in range(quarters):
-                first = (quarter if k == 0 else partner(quarter, quarters, k)) * piece
-                even, odd, _ = order_rows(pair_ref, slot, first, piece)
-                both = product(weighted, rows_of(rows, first, piece), (1, 1))
-                parts[unit, k, own] = jnp.where(
-                    even, both[:columns], jnp.where(odd, both[columns:], 0.0)
-                )
+            main = piece - piece % 128
+            rest = piece - main
+            firsts = [
+                (quarter if k == 0 else partner(quarter, quarters, k)) * piece
+                for k in range(quarters)
+            ]
+            ends = product(
+                weighted,
+                jnp.concatenate([rows_of(rows, first + main, rest) for first in firsts], axis=0),
+                (1, 1),
+            )
+            for k, first in enumerate(firsts):
+                both = product(weighted, rows_of(rows, first, main), (1, 1))
+                for start, size, sums in (
+                    (0, main, both), (main, rest, ends[:, k * rest : (k + 1) * rest])
+                ):
+                    even, odd, _ = order_rows(pair_ref, slot, first + start, size)
+                    parts[unit, k, own, :, start : start + size] = jnp.where(
+                        even, sums[:columns], jnp.where(odd, sums[columns:], 0.0)
+                    )
 
         def advance(unit):
             to_near(unit, 1).wait_recv()

time: 559 us -> 552 us (0.987)
  local copies, waits for them, and re-layouts: 20.7 us -> 12.3 us
    unnamed x16 -> x2, local copies, waits for them, and re-layouts: 16 us -> 7.59 us
where the time goes in v3:
time: 552 us; the launch traced here: 551 us
  Pallas kernels  527 us (95%)
  local copies, waits for them, and re-layouts  12.3 us (2%)
  other arithmetic  11.4 us (2%)
    pallas_call x1, Pallas kernels, synthesis(): pl.pallas_call(synthesis_kernel, in_specs=[pl.BlockSpec(memory_space=pltp...  261 us
    pallas_call x1, Pallas kernels, analysis(): pl.pallas_call(analysis_kernel, in_specs=[pl.BlockSpec(memory_space=pltpu...  240 us
    pallas_call x1, Pallas kernels, transport(): pl.pallas_call(transport_kernel, grid=(levels, count), in_specs=[smem, sm...  25.6 us

profile of v3, /device:TPU:12, one launch (start us, length us, event | category | flops | bytes accessed | tf_op | source)
XLA Modules:
  0.0 551.3 jit_solution(17200001909913803893)
XLA Ops:
  0.6 1.3 dynamic_slice.3.pair_ref
  2.0 0.7 broadcast_subtract_fusion
  2.7 1.4 copy.9.rate_ref
  4.0 0.2 sine_multiply_fusion.1
  4.3 2.1 fusion.13
  6.4 3.4 fusion.25
  9.8 0.2 subtract_dynamic-update-slice_fusion.15
  10.0 0.2 subtract_dynamic-update-slice_fusion.14
  10.2 0.2 subtract_dynamic-update-slice_fusion.13
  10.4 0.2 subtract_dynamic-update-slice_fusion.12
  10.6 0.2 subtract_dynamic-update-slice_fusion.11
  10.8 0.2 subtract_dynamic-update-slice_fusion.10
  11.0 0.2 subtract_dynamic-update-slice_fusion.9
  11.2 0.2 subtract_dynamic-update-slice_fusion.8
  11.5 0.3 pad_maximum_fusion.1
  11.8 0.2 subtract_dynamic-update-slice_fusion.7
  12.0 0.2 subtract_dynamic-update-slice_fusion.6
  12.2 0.2 subtract_dynamic-update-slice_fusion.5
  12.4 0.2 subtract_dynamic-update-slice_fusion.4
  12.6 0.2 subtract_dynamic-update-slice_fusion.3
  12.8 0.2 subtract_dynamic-update-slice_fusion.2
  13.0 0.2 subtract_dynamic-update-slice_fusion.1
  13.3 0.2 subtract_dynamic-update-slice_fusion
  13.5 0.3 pad_maximum_fusion.2
  13.8 4.5 fusion
  18.3 239.8 %shard_map.77 = (f32[1024,2048]{1,0:T(8,128)}, f32[4,32,2048]{2,1,0:T(8,128)}, f32[4,8,2048]{2,1,0:T(8,128)}, f32[4,8,2048]{2,1,0:T(8,128)}, f32[12,2,3,2048]{3,...) custom-call(s32[64]{0:T(128)} %dynamic_slice.3.pair_ref, f32[64,64,264]{2,1,0:T(8,128)} %bitcast.44, ...), custom_call_target="tpu_custom_call" | custom-call | tf_op jit(solution)/shard_map/pallas_call | solution.py:527
  258.1 25.6 %shard_map.78 = (f32[12,2,32,2048]{3,2,1,0:T(8,128)}, f32[2,32,2048]{2,1,0:T(8,128)}) custom-call(s32[1]{0:T(128)} %bitcast.first_ref, f32[12,2]{1,0:T(8,128)} %copy.9.rate_ref, f32[12,2,32,2048]{3,2,1,0:T(8,128)} %q_ref.1, f32[12,2,3,2048]{3,2,1,0:T(4,128)} %get-tuple-element.27.ql_ref, f32[12,2,3,2048]{3,2,1,0:T(4,128)} %get-tuple-element.28.qh_ref, ...), custom_call_target="tpu_custom_call" | custom-call | tf_op jit(solution)/shard_map/pallas_call | solution.py:177
  283.7 261.3 %shard_map.79 = (f32[64,64,264]{2,1,0:T(8,128)}, f32[8,8,256,128]{3,2,1,0:T(8,128)}) custom-call(s32[64]{0:T(128)} %dynamic_slice.3.pair_ref, f32[1,256]{1,0:T(1,128)} %quad_ref.1, f32[2,32,2048]{2,1,0:T(8,128)} %get-tuple-element.32.heat_ref, f32[1024,2048]{1,0:T(8,128)} %get-tuple-element.33.field_ref, bf16[2,1024,1024]{2,1,0:T(8,128)(2,1)} %get-tuple-element.39.high_ref, ...), custom_call_target="tpu_custom_call" | custom-call | tf_op jit(solution)/shard_map/pallas_call | solution.py:802
  545.0 6.2 %copy.39 = f32[64,264,64]{1,2,0:T(8,128)} copy(f32[64,264,64]{1,2,0:T(8,128)} %bitcast.45) | data formatting | bytes 8650752
  (3 shorter events, 0.1 us)
